TPU v7x, 32 devices: a whole 2x2x4 slice. The times are simulated.
32 devices in a mesh: section: 2 (over core), dp: 16 (over z, y, x).
Axes of the slice: x: 2, y: 2, z: 4, core: 2. Of those that a mesh axis runs over, the one named last changes fastest.
Arguments:
- tokens: bfloat16 [2, 16, 80, 1024], P(None, 'dp'), may hold values from -6 to 6
- w_qkv: bfloat16 [2, 1024, 1536], P('section', 'dp'), may hold values from -0.1875 to 0.1875
- w_output: bfloat16 [2, 512, 1024], P('section', None, 'dp'), may hold values from -0.25 to 0.25
- tangent_value: bfloat16 [2, 2, 1024, 512], P('section', None, 'dp'), may hold values from -0.1875 to 0.1875
- tangent_output: bfloat16 [2, 2, 512, 1024], P('section', None, None, 'dp'), may hold values from -0.25 to 0.25
- layer_gain: float32 [2, 1024], P('section'), may hold values from 0.5 to 1.5
- final_gain: float32 [1024], replicated, may hold values from 0.5 to 1.5
- head: bfloat16 [1024, 1000], P(None, 'section'), may hold values from -0.1875 to 0.1875
Outputs:
- mean_logits: float32 [2, 16, 1000], P(None, 'dp', 'section')
- variance: float32 [2, 16, 1000], P(None, 'dp', 'section')
All inputs are finite; a program needn't handle non-finite values.
Results may differ from a plain program's by a relative error of at most 0.018.
Values may be sent and summed in bfloat16 or wider, within the bound.
A program may use at most 64 MiB of HBM per device.

v0:
```python
import functools

import jax
import jax.numpy as jnp
from jax import lax
from jax.experimental import pallas as pl
from jax.experimental.pallas import tpu as pltpu
from jax.sharding import PartitionSpec as P

HEAD = 64
epsilon = 1e-06
F32, BF16 = jnp.float32, jnp.bfloat16
MESH = pl.DeviceIdType.MESH


def contract(spec, left, right):
    return jnp.einsum(spec, left, right, preferred_element_type=jnp.float32)


def norm_jvp(primal, tangents, gains):
    average = jnp.mean(primal, -1, keepdims=True)
    centred = primal - average
    inverse = lax.rsqrt(jnp.mean(centred * centred, -1, keepdims=True) + epsilon)
    dcentred = tangents - jnp.mean(tangents, -1, keepdims=True)
    dinverse = -(inverse**3) * jnp.mean(centred * dcentred, -1, keepdims=True)
    return (centred * inverse * gains, (dcentred * inverse + centred * dinverse) * gains)


def layer_step(state, qkv_weight, out_weight, value_tangent, out_tangent, gains):
    hd = out_weight.shape[0]
    heads = hd // HEAD
    resid = state.astype(F32)
    normed_zero, normed_rest = norm_jvp(resid[0], resid[1:], gains)
    normed = jnp.concatenate([normed_zero[None], normed_rest]).astype(BF16)
    streams, batch, tokens_here, width = normed.shape
    projected = contract("sbtd,de->sbte", normed, qkv_weight)
    extra_value = contract("btd,kde->kbte", normed[0], value_tangent)
    queries = projected[..., :hd]
    key_rows = projected[..., hd : 2 * hd]
    values = projected[..., 2 * hd :]
    values = jnp.concatenate([values[:1], values[1:] + extra_value])
    shape_heads = (streams, batch, tokens_here, heads, HEAD)
    queries = queries.astype(BF16).reshape(shape_heads)
    key_rows = key_rows.astype(BF16).reshape(shape_heads)
    values = values.astype(BF16).reshape(shape_heads)
    factor = HEAD ** (-0.5)
    scores = contract("bqhe,bkhe->bhqk", queries[0], key_rows[0]) * factor
    probs = jax.nn.softmax(scores, -1)
    dscores = (
        contract("sbqhe,bkhe->sbhqk", queries[1:], key_rows[0])
        + contract("bqhe,sbkhe->sbhqk", queries[0], key_rows[1:])
    ) * factor
    dprobs = probs * (dscores - jnp.sum(probs * dscores, -1, keepdims=True))
    probs_low = probs.astype(BF16)
    dprobs_low = dprobs.astype(BF16)
    attended_zero = contract("bhqk,bkhe->bqhe", probs_low, values[0])
    attended_rest = contract("sbhqk,bkhe->sbqhe", dprobs_low, values[0]) + contract(
        "bhqk,sbkhe->sbqhe", probs_low, values[1:]
    )
    attended = jnp.concatenate([attended_zero[None], attended_rest]).astype(BF16)
    attended = attended.reshape(streams, batch, tokens_here, hd)
    output = contract("sbte,ed->sbtd", attended, out_weight)
    extra_out = contract("bte,ked->kbtd", attended[0], out_tangent)
    output = jnp.concatenate([output[:1], output[1:] + extra_out])
    return (resid + output).astype(BF16)


def relay_shards(tokens, w_qkv, w_output, tangent_value, tangent_output, layer_gain, final_gain, head):
    full_qkv, full_output, full_value_tan, full_output_tan = (
        lax.all_gather(w_qkv, "dp", axis=1, tiled=True),
        lax.all_gather(w_output, "dp", axis=2, tiled=True),
        lax.all_gather(tangent_value, "dp", axis=2, tiled=True),
        lax.all_gather(tangent_output, "dp", axis=3, tiled=True),
    )
    tangents = tangent_value.shape[1]

    def advance_layer(state):
        return layer_step(
            state, full_qkv[0], full_output[0], full_value_tan[0], full_output_tan[0], layer_gain[0]
        )

    section_index = lax.axis_index("section")
    section_count = lax.axis_size("section")
    route = [(i, i + 1) for i in range(section_count - 1)]
    micro, _, toks, width = tokens.shape
    entering = jnp.concatenate(
        [tokens.reshape(1, micro, toks, width), jnp.zeros((tangents, micro, toks, width), BF16)]
    )

    def advance(step, outgoing):
        incoming = lax.ppermute(outgoing, "section", route)
        source = jnp.where(step == 0, entering, incoming)
        return lax.cond(section_index == step, advance_layer, jnp.zeros_like, source)

    finished = lax.fori_loop(0, section_count, advance, jnp.zeros_like(entering))
    collected = finished[:, :, 0, :]
    mine = section_index == section_count - 1
    features = lax.psum(jnp.where(mine, collected, jnp.zeros_like(collected)), "section")
    widened = features.astype(F32)
    final_zero, final_rest = norm_jvp(widened[0], widened[1:], final_gain)
    normed_final = jnp.concatenate([final_zero[None], final_rest]).astype(BF16)
    logits = contract("sbd,dc->sbc", normed_final, head)
    return (logits[0][:, None, :], jnp.sum(logits[1:] * logits[1:], 0)[:, None, :])


def dot(a, b):
    return lax.dot_general(a, b, (((1,), (0,)), ((), ())), preferred_element_type=F32)


def dot_t(a, b):
    return lax.dot_general(a, b, (((1,), (1,)), ((), ())), preferred_element_type=F32)


class Gather:
    def __init__(self, n, a_full, b_full, send, recv):
        self.nz = n // 4
        self.a_full, self.b_full, self.send, self.recv = a_full, b_full, send, recv
        self.rows = a_full.shape[0] // n
        self.me = lax.axis_index("dp")
        self.section = lax.axis_index("section")
        me = self.me
        self.x_near = me + 1 - 2 * (me % 2)
        self.y_near = me + 2 - 4 * ((me // 2) % 2)
        self.z = me // 4
        self.diagonal = self.x_near + self.y_near - me
        self.sends = []
        self.slot = 0

    def piece(self, src, group, half):
        depth = self.rows // 2
        at = pl.ds(pl.multiple_of(src * self.rows + half * depth, depth), depth)
        return self.a_full.at[at, :] if group == 0 else self.b_full.at[:, at, :]

    def copy(self, src, group, half, target, slot):
        ref = self.piece(src, group, half)
        return pltpu.make_async_remote_copy(
            src_ref=ref,
            dst_ref=ref,
            send_sem=self.send.at[slot],
            recv_sem=self.recv.at[src, group * 2 + half],
            device_id={"section": self.section, "dp": target},
            device_id_type=MESH,
        )

    def forward(self, cond, src, group, half, target):
        slot = self.slot
        self.slot += 1

        def go():
            self.copy(src, group, half, target, slot).start()

        def end():
            self.copy(src, group, half, target, slot).wait_send()

        if cond is None:
            go()
        else:
            pl.when(cond)(go)
        self.sends.append((cond, end))

    def arrived(self, src, group, half):
        self.copy(src, group, half, self.me, 0).wait_recv()

    def sources(self, d):
        if d == 0:
            return [(0, None)]
        return [(-d, self.z >= d), (d, self.z + d < self.nz)]

    def direct(self, group, d):
        for shift, cond in self.sources(d):
            src = self.me + 4 * shift
            for half in range(2):
                if d > 0:
                    pl.when(cond)(functools.partial(self.arrived, src, group, half))
                if shift <= 0 and d < self.nz - 1:
                    up = self.z + 1 < self.nz
                    self.forward(up if cond is None else cond & up, src, group, half, self.me + 4)
                if shift >= 0 and d < self.nz - 1:
                    down = self.z >= 1
                    self.forward(down if cond is None else cond & down, src, group, half, self.me - 4)
                order = ((self.y_near, self.x_near), (self.x_near, self.y_near))[half]
                for target in order:
                    self.forward(cond, src, group, half, target)

    def relay(self, group, d):
        for shift, cond in self.sources(d):
            for half, near, target in ((0, self.x_near, self.y_near), (1, self.y_near, self.x_near)):
                src = near + 4 * shift
                wait = functools.partial(self.arrived, src, group, half)
                wait() if cond is None else pl.when(cond)(wait)
                self.forward(cond, src, group, half, target)

    def rest(self, group):
        for z in range(self.nz):
            up = 4 * (z - self.z)
            self.arrived(self.x_near + up, group, 1)
            self.arrived(self.y_near + up, group, 0)
            self.arrived(self.diagonal + up, group, 0)
            self.arrived(self.diagonal + up, group, 1)

    def drain(self):
        for cond, end in self.sends:
            end() if cond is None else pl.when(cond)(end)
        self.sends = []


def send_slots(n):
    nz = n // 4
    return 2 * 2 * (4 + 3 * 2 * (nz - 1) + 2 * nz)


def norm_rows(x, gains):
    average = jnp.mean(x, -1, keepdims=True)
    centred = x - average
    inverse = lax.rsqrt(jnp.mean(centred * centred, -1, keepdims=True) + epsilon)
    return centred, inverse, centred * inverse * gains


def norm_tangent(t, centred, inverse, gains):
    dcentred = t - jnp.mean(t, -1, keepdims=True)
    dinverse = -(inverse * inverse * inverse) * jnp.mean(centred * dcentred, -1, keepdims=True)
    return (dcentred * inverse + centred * dinverse) * gains


def softmax(scores):
    e = jnp.exp(scores - jnp.max(scores, -1, keepdims=True))
    return e / jnp.sum(e, -1, keepdims=True)


def first_norm(sizes, tokens, gain, normed):
    micro, toks, width, hd, tangents = sizes
    for b in range(micro):
        x = tokens[b].astype(F32)
        normed[0, pl.ds(b * toks, toks), :] = norm_rows(x, gain[...])[2].astype(BF16)


def first_qkv(sizes, a_full, normed, proj):
    micro, toks, width, hd, tangents = sizes
    n = normed[0]
    for c in range(3 + tangents):
        at = pl.ds(c * hd, hd)
        proj[:, at] = dot(n, a_full[:, at]).astype(BF16)


def first_attend(sizes, proj, att, b):
    micro, toks, width, hd, tangents = sizes
    factor = HEAD ** (-0.5)
    even = lax.broadcasted_iota(jnp.int32, (toks, 2 * HEAD), 1) < HEAD
    rows = pl.ds(b * toks, toks)
    for pair in range(hd // (2 * HEAD)):
        lanes = pair * 2 * HEAD
        q = proj[rows, pl.ds(lanes, 2 * HEAD)]
        k = proj[rows, pl.ds(hd + lanes, 2 * HEAD)]
        vs = [proj[rows, pl.ds((2 + s) * hd + lanes, 2 * HEAD)] for s in range(1 + tangents)]
        zero = jnp.zeros_like(q)
        low = []
        for mine in (jnp.where(even, q, zero), jnp.where(even, zero, q)):
            low.append(softmax(dot_t(mine, k) * factor).astype(BF16))
        for s, v in enumerate(vs):
            joined = jnp.where(even, dot(low[0], v), dot(low[1], v))
            at = pl.ds((s * micro + b) * toks, toks)
            att[at, pl.ds(lanes, 2 * HEAD)] = joined.astype(BF16)


def first_out(sizes, tokens, b_full, att, state):
    micro, toks, width, hd, tangents = sizes
    rows0 = micro * toks
    tile = 256
    for c in range(width // tile):
        at = pl.ds(c * tile, tile)
        out = dot_t(att[...], b_full[0, at, :])
        extra = [dot_t(att[pl.ds(0, rows0), :], b_full[1 + j, at, :]) for j in range(tangents)]
        for b in range(micro):
            x = tokens[b, :, at].astype(F32)
            state[pl.ds(b * toks, toks), at] = (x + out[b * toks : (b + 1) * toks]).astype(BF16)
        for j in range(tangents):
            state[pl.ds((1 + j) * rows0, rows0), at] = (
                out[(1 + j) * rows0 : (2 + j) * rows0] + extra[j]
            ).astype(BF16)


BLOCK = 16


class Plane:
    def __init__(self, g, send, recv):
        self.g, self.send, self.recv = g, send, recv
        self.place = g.me % 4
        self.peers = (g.diagonal, g.x_near, g.y_near)

    def copy(self, stage, i, src, dst, source):
        return pltpu.make_async_remote_copy(
            src_ref=src,
            dst_ref=dst,
            send_sem=self.send.at[stage, i],
            recv_sem=self.recv.at[stage, source],
            device_id={"section": self.g.section, "dp": self.peers[i]},
            device_id_type=MESH,
        )

    def exchange(self, stage, out_of, into):
        for i, peer in enumerate(self.peers):
            self.copy(stage, i, out_of(peer % 4), into(self.place), self.place).start()

    def arrive(self, stage, out_of, into):
        for i, peer in enumerate(self.peers):
            self.copy(stage, i, out_of(peer % 4), into(peer % 4), peer % 4).wait_recv()

    def finish(self, stage, out_of, into):
        for i, peer in enumerate(self.peers):
            self.copy(stage, i, out_of(peer % 4), into(self.place), self.place).wait_send()


class Line:
    def __init__(self, g, parts, send, recv):
        self.g, self.parts, self.send, self.recv = g, parts, send, recv
        self.sends = []

    def copy(self, z, group, way, target):
        rows = 4 * self.g.rows
        at = pl.ds(pl.multiple_of(z * rows, rows), rows)
        ref = self.parts[0].at[at, :] if group == 0 else self.parts[1].at[:, at, :]
        return pltpu.make_async_remote_copy(
            src_ref=ref,
            dst_ref=ref,
            send_sem=self.send.at[z, 2 * group + way],
            recv_sem=self.recv.at[z, group],
            device_id={"section": self.g.section, "dp": target},
            device_id_type=MESH,
        )

    def run(self, group):
        g = self.g
        for d in range(g.nz):
            for shift, cond in g.sources(d):
                z = g.z + shift

                def step(z=z, shift=shift, d=d):
                    if d > 0:
                        self.copy(z, group, 0, g.me).wait_recv()
                    if shift <= 0 and d < g.nz - 1:
                        pl.when(g.z + 1 < g.nz)(lambda: self.copy(z, group, 0, g.me + 4).start())
                    if shift >= 0 and d < g.nz - 1:
                        pl.when(g.z >= 1)(lambda: self.copy(z, group, 1, g.me - 4).start())

                step() if cond is None else pl.when(cond)(step)

    def drain(self, group):
        g = self.g
        for d in range(g.nz - 1):
            for shift, cond in g.sources(d):
                z = g.z + shift

                def step(z=z, shift=shift):
                    if shift <= 0:
                        pl.when(g.z + 1 < g.nz)(lambda: self.copy(z, group, 0, g.me + 4).wait_send())
                    if shift >= 0:
                        pl.when(g.z >= 1)(lambda: self.copy(z, group, 1, g.me - 4).wait_send())

                step() if cond is None else pl.when(cond)(step)


def class_rows(sizes, gain, state):
    micro, toks, width, hd, tangents = sizes
    streams = 1 + tangents
    rows0 = micro * toks
    filler = [jnp.zeros((BLOCK - micro * streams, width), F32)]
    heads_of = [
        state[pl.ds(s * rows0 + b * toks, 16), :].astype(F32)[:1] for s in range(streams) for b in range(micro)
    ]
    resid = jnp.concatenate(heads_of + filler, 0)
    primal = jnp.concatenate(heads_of[:micro] * streams + filler, 0)
    centred, inverse, y = norm_rows(primal, gain[...])
    dy = norm_tangent(resid, centred, inverse, gain[...])
    which = lax.broadcasted_iota(jnp.int32, resid.shape, 0)
    return resid, jnp.where(which < micro, y, dy).astype(BF16)


def last_norm(sizes, gain, state, normed):
    micro, toks, width, hd, tangents = sizes
    rows0 = micro * toks
    for b in range(micro):
        at = pl.ds(b * toks, toks)
        centred, inverse, y = norm_rows(state[at, :].astype(F32), gain[...])
        normed[0, at, :] = y.astype(BF16)
        for j in range(tangents):
            t = state[pl.ds((1 + j) * rows0 + b * toks, toks), :].astype(F32)
            normed[1 + j, at, :] = norm_tangent(t, centred, inverse, gain[...]).astype(BF16)


def last_attend(sizes, heads, u, normed):
    micro, toks, width, hd, tangents = sizes
    streams = 1 + tangents
    factor = HEAD ** (-0.5)
    sums = []
    for b in range(micro):
        at = pl.ds(b * toks, toks)
        ub = u[b * streams * heads : (b + 1) * streams * heads].astype(BF16)
        base = dot_t(ub, normed[0, at, :]) * factor
        u0 = ub[:heads]
        probs = softmax(base[:heads])
        weights = [probs]
        for j in range(tangents):
            ds = base[(1 + j) * heads : (2 + j) * heads] + dot_t(u0, normed[1 + j, at, :]) * factor
            weights.append(probs * (ds - jnp.sum(probs * ds, -1, keepdims=True)))
        m = dot(jnp.concatenate(weights, 0).astype(BF16), normed[0, at, :])
        low = probs.astype(BF16)
        parts = [m[:heads]]
        for j in range(tangents):
            parts.append(m[(1 + j) * heads : (2 + j) * heads] + dot(low, normed[1 + j, at, :]))
        sums += parts
    return jnp.concatenate(sums, 0).astype(BF16)


def order(sizes, heads, flip):
    micro, toks, width, hd, tangents = sizes
    streams = 1 + tangents
    share = heads // 4
    few, many = micro * streams * heads, heads * BLOCK
    shape = (many, few) if flip else (few, many)
    r = lax.broadcasted_iota(jnp.int32, shape, 1 if flip else 0)
    c = lax.broadcasted_iota(jnp.int32, shape, 0 if flip else 1)
    head, i = r % heads, r // heads
    i = (i % streams) * micro + i // streams
    return (c == head * BLOCK + i).astype(F32).astype(BF16)


def lowered(extra, micro, rows):
    width = extra[0].shape[-1]
    parts = [jnp.zeros((micro, width), F32)] + [e[:micro] for e in extra]
    used = micro * len(parts)
    return jnp.concatenate(parts + [jnp.zeros((rows - used, width), F32)], 0)


def kernel(
    n, sizes, tokens, w_qkv, tangent_value, outs, gain, final_gain, head, mean_ref, var_ref,
    a_full, b_full, normed, proj, att, state, state_in, classes, classes_in,
    a_quarter, b_quarter, a_part, b_part, cls_all, u_out, u_all, m_out, m_all, o_out, o_all,
    send, recv, local, gate, core_sems, plane_send, plane_recv, line_send, line_recv,
):
    micro, toks, width, hd, tangents = sizes
    streams = 1 + tangents
    heads = hd // HEAD
    share = heads // 4
    part = share * HEAD
    g = Gather(n, a_full, b_full, send, recv)
    me, section = g.me, g.section
    other = 1 - section
    up, down = g.z + 1 < g.nz, g.z >= 1
    plane = Plane(g, plane_send, plane_recv)
    line = Line(g, (a_part, b_part), line_send, line_recv)

    barrier = pltpu.get_barrier_semaphore()

    def greet(target, sec):
        pl.semaphore_signal(
            barrier, inc=1, device_id={"section": sec, "dp": target}, device_id_type=MESH
        )

    for near in (g.x_near, g.y_near, g.diagonal):
        greet(near, section)
    greet(me, other)
    pl.when(up)(lambda: greet(me + 4, section))
    pl.when(down)(lambda: greet(me - 4, section))

    def met():
        if g.nz > 1:
            middle = up & down
            pl.when(middle)(lambda: pl.semaphore_wait(barrier, 6))
            pl.when(jnp.logical_not(middle))(lambda: pl.semaphore_wait(barrier, 5))
        else:
            pl.semaphore_wait(barrier, 4)

    def across(src, dst, i):
        return pltpu.make_async_remote_copy(
            src_ref=src,
            dst_ref=dst,
            send_sem=core_sems.at[2 * i],
            recv_sem=core_sems.at[2 * i + 1],
            device_id={"section": other, "dp": me},
            device_id_type=MESH,
        )

    own = pl.ds(pl.multiple_of(me * g.rows, g.rows), g.rows)

    def moved(pairs):
        moves = [pltpu.make_async_copy(src, dst, local.at[i]) for i, (src, dst) in enumerate(pairs)]
        for move in moves:
            move.start()
        for move in moves:
            move.wait()

    met()

    @pl.when(section == 0)
    def _():
        pairs = [(w_qkv, a_full.at[own, pl.ds(0, 3 * hd)])]
        for j in range(tangents):
            pairs.append((tangent_value.at[j], a_full.at[own, pl.ds((3 + j) * hd, hd)]))
        pairs.append((outs, b_full.at[:, own, :]))
        moved(pairs)
        steps = [(group, d) for group in range(2) for d in range(g.nz)]
        lag = 2
        chunks = [
            lambda: (g.rest(0), first_qkv(sizes, a_full, normed, proj)),
            *[functools.partial(first_attend, sizes, proj, att, b) for b in range(micro)],
        ]
        for i in range(len(steps) + lag):
            if i < len(steps):
                g.direct(*steps[i])
            if i == 0:
                first_norm(sizes, tokens, gain, normed)
            if i == 0:
                pl.semaphore_signal(
                    gate, inc=1, device_id={"section": other, "dp": me}, device_id_type=MESH
                )
            if i >= lag:
                g.relay(*steps[i - lag])
            if i >= len(steps) - 1 and i < len(steps) + lag - 1 and chunks:
                chunks.pop(0)()
        for chunk in chunks:
            chunk()
        g.rest(1)
        first_out(sizes, tokens, b_full, att, state)
        onward = across(state, state_in, 0)
        onward.start()
        g.drain()
        onward.wait_send()
        across(classes, classes_in, 1).wait_recv()

    @pl.when(section == 1)
    def _():
        pairs = []
        for p in range(4):
            for m in range(3):
                pairs.append(
                    (w_qkv.at[:, pl.ds(m * hd + p * part, part)], a_quarter.at[p, :, pl.ds(m * part, part)])
                )
            for j in range(tangents):
                pairs.append(
                    (
                        tangent_value.at[j, :, pl.ds(p * part, part)],
                        a_quarter.at[p, :, pl.ds((3 + j) * part, part)],
                    )
                )
            pairs.append((outs.at[:, :, pl.ds(p * part, part)], b_quarter.at[p]))
        moved(pairs)

        def at_place(place):
            row = (g.z * 4 + place) * g.rows
            return pl.ds(pl.multiple_of(row, g.rows), g.rows)

        stages = [
            (0, lambda p: a_quarter.at[p], lambda p: a_part.at[at_place(p), :]),
            (1, lambda p: b_quarter.at[p], lambda p: b_part.at[:, at_place(p), :]),
            (2, lambda p: cls_all.at[plane.place], lambda p: cls_all.at[p]),
            (3, lambda p: u_out.at[p], lambda p: u_all.at[p]),
            (4, lambda p: m_out.at[p], lambda p: m_all.at[p]),
            (5, lambda p: o_out.at[p], lambda p: o_all.at[p]),
        ]
        for stage in stages[:2]:
            plane.exchange(*stage)
        moved(
            [
                (a_quarter.at[plane.place], a_part.at[own, :]),
                (b_quarter.at[plane.place], b_part.at[:, own, :]),
            ]
        )
        for stage in stages[:2]:
            plane.arrive(*stage)
        pl.semaphore_wait(gate, 1)
        line.run(0)
        line.run(1)

        across(state, state_in, 0).wait_recv()
        resid, firsts = class_rows(sizes, gain, state_in)
        cls_all[plane.place] = firsts
        plane.exchange(*stages[2])
        last_norm(sizes, gain, state_in, normed)
        plane.arrive(*stages[2])
        rows = jnp.concatenate([cls_all[k] for k in range(4)], 0)
        q = dot(rows, a_part[:, pl.ds(0, part)]).astype(BF16)
        owner = lax.broadcasted_iota(jnp.int32, (BLOCK, part), 1) // HEAD
        zero = jnp.zeros((BLOCK, part), F32)
        spread = []
        for k in range(4):
            block = q[k * BLOCK : (k + 1) * BLOCK].astype(F32)
            spread += [jnp.where(owner == h, block, zero) for h in range(share)]
        u = dot_t(jnp.concatenate(spread, 0).astype(BF16), a_part[:, pl.ds(part, part)]).astype(BF16)
        tall = share * BLOCK
        for k in range(4):
            u_out[k] = u[k * tall : (k + 1) * tall]
        plane.exchange(*stages[3])
        u_all[plane.place] = u_out[plane.place]
        plane.arrive(*stages[3])
        u48 = dot(order(sizes, heads, False), jnp.concatenate([u_all[k] for k in range(4)], 0))
        sums = last_attend(sizes, heads, u48, normed)
        spreadm = dot(order(sizes, heads, True), sums).astype(BF16)
        for k in range(4):
            m_out[k] = spreadm[k * tall : (k + 1) * tall]
        plane.exchange(*stages[4])
        m_all[plane.place] = m_out[plane.place]
        plane.arrive(*stages[4])
        m = jnp.concatenate([m_all[k] for k in range(4)], 0)
        r = [dot(m, a_part[:, pl.ds((2 + c) * part, part)]) for c in range(streams)]

        def picked(x, k):
            chosen = zero
            for h in range(share):
                at = k * tall + h * BLOCK
                chosen = jnp.where(owner == h, x[at : at + BLOCK], chosen)
            return chosen

        attended = jnp.concatenate(
            [
                picked(r[0], k) + lowered([picked(x, k) for x in r[1:]], micro, BLOCK)
                for k in range(4)
            ],
            0,
        ).astype(BF16)
        out = [dot_t(attended, b_part[c]) for c in range(streams)]
        some = o_out.shape[1]
        for k in range(4):
            at = k * BLOCK
            extra = [x[at : at + micro] for x in out[1:]]
            o_out[k] = out[0][at : at + some] + lowered(extra, micro, some)
        plane.exchange(*stages[5])
        o_all[plane.place] = o_out[plane.place]
        plane.arrive(*stages[5])
        total = o_all[0] + o_all[1] + o_all[2] + o_all[3]
        final = (resid[:some] + total).astype(BF16).astype(F32)
        classes[...] = final
        back = across(classes, classes_in, 1)
        back.start()
        classes_in[...] = final
        for stage in stages:
            plane.finish(*stage)
        line.drain(0)
        line.drain(1)
        back.wait_send()

    rows = classes_in[...]
    count = classes_in.shape[0]
    primal = jnp.concatenate([rows[:micro]] * (1 + tangents) + [rows[(1 + tangents) * micro :]], 0)
    centred, inverse, y = norm_rows(primal, final_gain[...])
    dy = norm_tangent(rows, centred, inverse, final_gain[...])
    which = lax.broadcasted_iota(jnp.int32, (count, width), 0)
    logits = dot_t(jnp.where(which < micro, y, dy).astype(BF16), head[...])
    mean_ref[:, 0, :] = logits[:micro]
    var_ref[:, 0, :] = sum(
        logits[(1 + j) * micro : (2 + j) * micro] * logits[(1 + j) * micro : (2 + j) * micro]
        for j in range(tangents)
    )


def two_sections(n):
    def shards(tokens, w_qkv, w_output, tangent_value, tangent_output, layer_gain, final_gain, head):
        micro, _, toks, width = tokens.shape
        tangents = tangent_value.shape[1]
        hd = w_output.shape[1]
        classes = head.shape[1]
        rows = width // n
        outs = jnp.swapaxes(jnp.concatenate([w_output, tangent_output[0]], 0), 1, 2)
        sizes = (micro, toks, width, hd, tangents)
        vmem = pl.BlockSpec(memory_space=pltpu.VMEM)
        anywhere = pl.BlockSpec(memory_space=pl.ANY)
        streams = 1 + tangents
        padded = -(-micro * streams // 8) * 8
        all_rows = streams * micro * toks
        tall = hd // HEAD // 4 * BLOCK
        mean, var = pl.pallas_call(
            functools.partial(kernel, n, sizes),
            out_shape=[jax.ShapeDtypeStruct((micro, 1, classes), F32)] * 2,
            in_specs=[vmem, anywhere, anywhere, anywhere, vmem, vmem, vmem],
            out_specs=[vmem, vmem],
            scratch_shapes=[
                pltpu.VMEM((width, (3 + tangents) * hd), BF16),
                pltpu.VMEM((streams, width, hd), BF16),
                pltpu.VMEM((streams, micro * toks, width), BF16),
                pltpu.VMEM((micro * toks, (3 + tangents) * hd), BF16),
                pltpu.VMEM((all_rows, hd), BF16),
                pltpu.VMEM((all_rows, width), BF16),
                pltpu.VMEM((all_rows, width), BF16),
                pltpu.VMEM((padded, width), F32),
                pltpu.VMEM((padded, width), F32),
                pltpu.VMEM((4, rows, (3 + tangents) * hd // 4), BF16),
                pltpu.VMEM((4, streams, rows, hd // 4), BF16),
                pltpu.VMEM((width, (3 + tangents) * hd // 4), BF16),
                pltpu.VMEM((streams, width, hd // 4), BF16),
                pltpu.VMEM((4, BLOCK, width), BF16),
                pltpu.VMEM((4, tall, width), BF16),
                pltpu.VMEM((4, tall, width), BF16),
                pltpu.VMEM((4, tall, width), BF16),
                pltpu.VMEM((4, tall, width), BF16),
                pltpu.VMEM((4, padded, width), F32),
                pltpu.VMEM((4, padded, width), F32),
                pltpu.SemaphoreType.DMA((send_slots(n),)),
                pltpu.SemaphoreType.DMA((n, 4)),
                pltpu.SemaphoreType.DMA((4 * (4 + tangents),)),
                pltpu.SemaphoreType.REGULAR,
                pltpu.SemaphoreType.DMA((4,)),
                pltpu.SemaphoreType.DMA((6, 3)),
                pltpu.SemaphoreType.DMA((6, 4)),
                pltpu.SemaphoreType.DMA((n // 4, 4)),
                pltpu.SemaphoreType.DMA((n // 4, 2)),
            ],
            compiler_params=pltpu.CompilerParams(
                collective_id=0, has_side_effects=True, vmem_limit_bytes=60 * 2**20
            ),
        )(
            tokens.reshape(micro, toks, width),
            w_qkv[0],
            tangent_value[0],
            outs,
            layer_gain,
            final_gain[None],
            head.T,
        )
        return mean, var

    return shards


def solution(mesh):
    n = mesh.shape["dp"]
    fast = mesh.shape["section"] == 2 and n % 4 == 0
    return jax.shard_map(
        two_sections(n) if fast else relay_shards,
        mesh=mesh,
        in_specs=(
            P(None, "dp", None, None),
            P("section", "dp", None),
            P("section", None, "dp"),
            P("section", None, "dp", None),
            P("section", None, None, "dp"),
            P("section", None),
            P(),
            P(None, "section"),
        ),
        out_specs=(P(None, "dp", "section"), P(None, "dp", "section")),
        check_vma=False,
    )
```

profile of v0, /device:TPU:0, one launch (start us, length us, event | category | flops | bytes accessed | tf_op | source)
XLA Modules:
  0.0 76.8 jit_solution(4323439476196258249)
XLA Ops:
  0.6 1.6 %maximum_bitcast_fusion.outs = bf16[3,64,512]{2,1,0:T(8,128)(2,1)} fusion(bf16[2,512,64]{1,2,0:T(8,128)(2,1)} %bitcast.11, bf16[1,512,64]{1,2,0:T(8,128)(2,1)} %param.10), kind=kLoop, calls=%fused_computation | loop fusion | flops 98304 | bytes 393216 | tf_op jit(solution)/shard_map/transpose | solution.py:663
  2.2 72.7 %shard_map.95 = (f32[2,1,500]{2,1,0:T(1,128)}, f32[2,1,500]{2,1,0:T(1,128)}) custom-call(bf16[2,80,1024]{2,1,0:T(8,128)(2,1)} %bitcast.9, bf16[64,1536]{1,0:T(8,128)(2,1)} %bitcast.10, bf16[2,64,512]{2,1,0:T(8,128)(2,1)} %bitcast.12, bf16[3,64,512]{2,1,0:T(8,128)(2,1)} %maximum_bitcast_fusion.outs, f32[1,1024]{1,0:T(1,128)} %gain.1, f32[1,1024]{1,0:T(1,128)} %bitcast.13, ...), custom_call_target="tpu_custom_call" | custom-call | tf_op jit(solution)/shard_map/pallas_call | solution.py:671
  74.9 0.0 copy-start
  74.9 1.3 %copy.12 = f32[2,1,500]{2,1,0:T(1,128)} copy(f32[2,1,500]{2,1,0:T(1,128)} %get-tuple-element.4) | data formatting | bytes 8000
  76.2 0.0 copy-done
  76.2 0.6 copy.13
Async XLA Ops:
  74.9 1.3 %copy-start = (f32[2,1,500]{2,1,0:T(1,128)S(1)}, f32[2,1,500]{2,1,0:T(1,128)}, u32[]{:S(2)}) copy-start(f32[2,1,500]{2,1,0:T(1,128)} %get-tuple-element.5) | copy-start | bytes 12004
where the time goes:
time: 77 us; the launch traced here: 76.8 us
  Pallas kernels  72.7 us (94%)
  local copies, waits for them, and re-layouts  1.87 us (2%)
  other arithmetic  1.59 us (2%)
    pallas_call x1, Pallas kernels, shards(): pl.pallas_call(functools.partial(kernel, n, sizes), out_shape=[jax.ShapeD...  72.7 us
    unnamed x4, local copies, waits for them, and re-layouts  1.87 us
    transpose x1, other arithmetic, shards(): outs = jnp.swapaxes(jnp.concatenate([w_output, tangent_output[0]], 0), 1, 2)  1.59 us

commit v1 on v0

v1 whole, which is shorter than its diff:
```python
import functools

import jax
import jax.numpy as jnp
from jax import lax
from jax.experimental import pallas as pl
from jax.experimental.pallas import tpu as pltpu
from jax.sharding import PartitionSpec as P

HEAD = 64
epsilon = 1e-06
F32, BF16 = jnp.float32, jnp.bfloat16
MESH = pl.DeviceIdType.MESH


def contract(spec, left, right):
    return jnp.einsum(spec, left, right, preferred_element_type=jnp.float32)


def norm_jvp(primal, tangents, gains):
    average = jnp.mean(primal, -1, keepdims=True)
    centred = primal - average
    inverse = lax.rsqrt(jnp.mean(centred * centred, -1, keepdims=True) + epsilon)
    dcentred = tangents - jnp.mean(tangents, -1, keepdims=True)
    dinverse = -(inverse**3) * jnp.mean(centred * dcentred, -1, keepdims=True)
    return (centred * inverse * gains, (dcentred * inverse + centred * dinverse) * gains)


def layer_step(state, qkv_weight, out_weight, value_tangent, out_tangent, gains):
    hd = out_weight.shape[0]
    heads = hd // HEAD
    resid = state.astype(F32)
    normed_zero, normed_rest = norm_jvp(resid[0], resid[1:], gains)
    normed = jnp.concatenate([normed_zero[None], normed_rest]).astype(BF16)
    streams, batch, tokens_here, width = normed.shape
    projected = contract("sbtd,de->sbte", normed, qkv_weight)
    extra_value = contract("btd,kde->kbte", normed[0], value_tangent)
    queries = projected[..., :hd]
    key_rows = projected[..., hd : 2 * hd]
    values = projected[..., 2 * hd :]
    values = jnp.concatenate([values[:1], values[1:] + extra_value])
    shape_heads = (streams, batch, tokens_here, heads, HEAD)
    queries = queries.astype(BF16).reshape(shape_heads)
    key_rows = key_rows.astype(BF16).reshape(shape_heads)
    values = values.astype(BF16).reshape(shape_heads)
    factor = HEAD ** (-0.5)
    scores = contract("bqhe,bkhe->bhqk", queries[0], key_rows[0]) * factor
    probs = jax.nn.softmax(scores, -1)
    dscores = (
        contract("sbqhe,bkhe->sbhqk", queries[1:], key_rows[0])
        + contract("bqhe,sbkhe->sbhqk", queries[0], key_rows[1:])
    ) * factor
    dprobs = probs * (dscores - jnp.sum(probs * dscores, -1, keepdims=True))
    probs_low = probs.astype(BF16)
    dprobs_low = dprobs.astype(BF16)
    attended_zero = contract("bhqk,bkhe->bqhe", probs_low, values[0])
    attended_rest = contract("sbhqk,bkhe->sbqhe", dprobs_low, values[0]) + contract(
        "bhqk,sbkhe->sbqhe", probs_low, values[1:]
    )
    attended = jnp.concatenate([attended_zero[None], attended_rest]).astype(BF16)
    attended = attended.reshape(streams, batch, tokens_here, hd)
    output = contract("sbte,ed->sbtd", attended, out_weight)
    extra_out = contract("bte,ked->kbtd", attended[0], out_tangent)
    output = jnp.concatenate([output[:1], output[1:] + extra_out])
    return (resid + output).astype(BF16)


def relay_shards(tokens, w_qkv, w_output, tangent_value, tangent_output, layer_gain, final_gain, head):
    full_qkv, full_output, full_value_tan, full_output_tan = (
        lax.all_gather(w_qkv, "dp", axis=1, tiled=True),
        lax.all_gather(w_output, "dp", axis=2, tiled=True),
        lax.all_gather(tangent_value, "dp", axis=2, tiled=True),
        lax.all_gather(tangent_output, "dp", axis=3, tiled=True),
    )
    tangents = tangent_value.shape[1]

    def advance_layer(state):
        return layer_step(
            state, full_qkv[0], full_output[0], full_value_tan[0], full_output_tan[0], layer_gain[0]
        )

    section_index = lax.axis_index("section")
    section_count = lax.axis_size("section")
    route = [(i, i + 1) for i in range(section_count - 1)]
    micro, _, toks, width = tokens.shape
    entering = jnp.concatenate(
        [tokens.reshape(1, micro, toks, width), jnp.zeros((tangents, micro, toks, width), BF16)]
    )

    def advance(step, outgoing):
        incoming = lax.ppermute(outgoing, "section", route)
        source = jnp.where(step == 0, entering, incoming)
        return lax.cond(section_index == step, advance_layer, jnp.zeros_like, source)

    finished = lax.fori_loop(0, section_count, advance, jnp.zeros_like(entering))
    collected = finished[:, :, 0, :]
    mine = section_index == section_count - 1
    features = lax.psum(jnp.where(mine, collected, jnp.zeros_like(collected)), "section")
    widened = features.astype(F32)
    final_zero, final_rest = norm_jvp(widened[0], widened[1:], final_gain)
    normed_final = jnp.concatenate([final_zero[None], final_rest]).astype(BF16)
    logits = contract("sbd,dc->sbc", normed_final, head)
    return (logits[0][:, None, :], jnp.sum(logits[1:] * logits[1:], 0)[:, None, :])


def dot(a, b):
    return lax.dot_general(a, b, (((1,), (0,)), ((), ())), preferred_element_type=F32)


def dot_t(a, b):
    return lax.dot_general(a, b, (((1,), (1,)), ((), ())), preferred_element_type=F32)


class Gather:
    def __init__(self, n, g, full, send, recv):
        self.nz = n // 4
        self.full, self.send, self.recv = full, send, recv
        self.rows = full.shape[1] // n
        self.g = g
        self.sends = []
        self.slot = 0

    def copy(self, src, half, target, slot):
        depth = self.rows // 2
        at = pl.ds(pl.multiple_of(src * self.rows + half * depth, depth), depth)
        ref = self.full.at[:, at, :]
        return pltpu.make_async_remote_copy(
            src_ref=ref,
            dst_ref=ref,
            send_sem=self.send.at[slot],
            recv_sem=self.recv.at[src, half],
            device_id={"section": self.g.section, "dp": target},
            device_id_type=MESH,
        )

    def forward(self, cond, src, half, target):
        slot = self.slot
        self.slot += 1

        def go():
            self.copy(src, half, target, slot).start()

        def end():
            self.copy(src, half, target, slot).wait_send()

        go() if cond is None else pl.when(cond)(go)
        self.sends.append((cond, end))

    def arrived(self, src, half):
        self.copy(src, half, self.g.me, 0).wait_recv()

    def direct(self, d):
        g = self.g
        for shift, cond in g.sources(d):
            src = g.me + 4 * shift
            for half in range(2):
                if d > 0:
                    pl.when(cond)(functools.partial(self.arrived, src, half))
                if shift <= 0 and d < self.nz - 1:
                    self.forward(g.up if cond is None else cond & g.up, src, half, g.me + 4)
                if shift >= 0 and d < self.nz - 1:
                    self.forward(g.down if cond is None else cond & g.down, src, half, g.me - 4)
                for target in ((g.y_near, g.x_near), (g.x_near, g.y_near))[half]:
                    self.forward(cond, src, half, target)

    def relay(self, d):
        g = self.g
        for shift, cond in g.sources(d):
            for half, near, target in ((0, g.x_near, g.y_near), (1, g.y_near, g.x_near)):
                src = near + 4 * shift
                wait = functools.partial(self.arrived, src, half)
                wait() if cond is None else pl.when(cond)(wait)
                self.forward(cond, src, half, target)

    def rest(self):
        g = self.g
        for z in range(self.nz):
            up = 4 * (z - g.z)
            self.arrived(g.x_near + up, 1)
            self.arrived(g.y_near + up, 0)
            self.arrived(g.diagonal + up, 0)
            self.arrived(g.diagonal + up, 1)

    def drain(self):
        for cond, end in self.sends:
            end() if cond is None else pl.when(cond)(end)


def send_slots(n):
    nz = n // 4
    return 2 * (4 + 3 * 2 * (nz - 1) + 2 * nz)


class Place:
    def __init__(self, n):
        self.nz = n // 4
        self.me = lax.axis_index("dp")
        self.section = lax.axis_index("section")
        me = self.me
        self.x_near = me + 1 - 2 * (me % 2)
        self.y_near = me + 2 - 4 * ((me // 2) % 2)
        self.diagonal = self.x_near + self.y_near - me
        self.z = me // 4
        self.place = me % 4
        self.up, self.down = self.z + 1 < self.nz, self.z >= 1
        self.plane = (me, self.x_near, self.y_near, self.diagonal)

    def sources(self, d):
        if d == 0:
            return [(0, None)]
        return [(-d, self.z >= d), (d, self.z + d < self.nz)]


def norm_rows(x, gains):
    average = jnp.mean(x, -1, keepdims=True)
    centred = x - average
    inverse = lax.rsqrt(jnp.mean(centred * centred, -1, keepdims=True) + epsilon)
    return centred, inverse, centred * inverse * gains


def norm_tangent(t, centred, inverse, gains):
    dcentred = t - jnp.mean(t, -1, keepdims=True)
    dinverse = -(inverse * inverse * inverse) * jnp.mean(centred * dcentred, -1, keepdims=True)
    return (dcentred * inverse + centred * dinverse) * gains


def softmax(scores):
    e = jnp.exp(scores - jnp.max(scores, -1, keepdims=True))
    return e / jnp.sum(e, -1, keepdims=True)


def at_rows(i, count):
    return pl.ds(pl.multiple_of(i * count, count), count)


def first_norm(sizes, tok, gain, normed, slot):
    micro, toks, width, hd, tangents = sizes
    for b in range(micro):
        x = tok[slot, pl.ds(b * toks, toks), :].astype(F32)
        normed[at_rows(slot * micro + b, toks), :] = norm_rows(x, gain)[2].astype(BF16)


def first_attend(sizes, acc, att, slot, b):
    micro, toks, width, hd, tangents = sizes
    factor = HEAD ** (-0.5)
    part = 2 * HEAD
    streams = 1 + tangents
    even = lax.broadcasted_iota(jnp.int32, (toks, part), 1) < HEAD
    rows = at_rows(slot * micro + b, toks)
    q = acc[rows, pl.ds(0, part)]
    k = acc[rows, pl.ds(part, part)].astype(BF16)
    v = acc[rows, pl.ds(2 * part, streams * part)].astype(BF16)
    zero = jnp.zeros_like(q)
    both = jnp.concatenate([jnp.where(even, q, zero), jnp.where(even, zero, q)], 0).astype(BF16)
    low = softmax(dot_t(both, k) * factor).astype(BF16)
    out = dot(low, v)
    for s in range(streams):
        joined = jnp.where(even, out[:toks, s * part : (s + 1) * part], out[toks:, s * part : (s + 1) * part])
        att[slot, pl.ds((s * micro + b) * toks, toks), :] = joined.astype(BF16)


def first_out(sizes, tok, place, b_full, att, state):
    micro, toks, width, hd, tangents = sizes
    rows0 = micro * toks
    tile = 256
    for c in range(width // tile):
        at = pl.ds(c * tile, tile)
        out = dot_t(att[...], b_full[0, at, :])
        extra = [dot_t(att[pl.ds(0, rows0), :], b_full[1 + j, at, :]) for j in range(tangents)]
        x = tok[place, :, at].astype(F32)
        state[pl.ds(0, rows0), at] = (x + out[:rows0]).astype(BF16)
        for j in range(tangents):
            state[pl.ds((1 + j) * rows0, rows0), at] = (
                out[(1 + j) * rows0 : (2 + j) * rows0] + extra[j]
            ).astype(BF16)


def group_of(sizes):
    micro, toks, width, hd, tangents = sizes
    return -(-micro * (1 + tangents) // 8) * 8


def stream_of(sizes, shape):
    return (lax.broadcasted_iota(jnp.int32, shape, 0) % group_of(sizes)) // sizes[0]


def lowered(sizes, parts):
    micro, tangents = sizes[0], sizes[4]
    stream = stream_of(sizes, parts[0].shape)
    total = parts[0]
    for j in range(tangents):
        moved = pltpu.roll(parts[1 + j], micro * (1 + j), 0)
        total = total + jnp.where(stream == 1 + j, moved, jnp.zeros_like(moved))
    return total


def primal_rows(sizes, x):
    micro, tangents = sizes[0], sizes[4]
    stream = stream_of(sizes, x.shape)
    spread = x
    for j in range(tangents):
        spread = jnp.where(stream == 1 + j, pltpu.roll(x, micro * (1 + j), 0), spread)
    return spread


def norm_group(sizes, x, gains):
    stream = stream_of(sizes, x.shape)
    centred, inverse, y = norm_rows(primal_rows(sizes, x), gains)
    dy = norm_tangent(x, centred, inverse, gains)
    return jnp.where(stream == 0, y, dy).astype(BF16)


def class_rows(sizes, state):
    micro, toks, width, hd, tangents = sizes
    streams = 1 + tangents
    rows = [
        state[pl.ds((s * micro + b) * toks, 16), :].astype(F32)[:1] for s in range(streams) for b in range(micro)
    ]
    return jnp.concatenate(rows + [jnp.zeros((group_of(sizes) - micro * streams, width), F32)], 0)


def last_norm(sizes, gain, state, normed):
    micro, toks, width, hd, tangents = sizes
    rows0 = micro * toks
    for b in range(micro):
        at = pl.ds(b * toks, toks)
        centred, inverse, y = norm_rows(state[at, :].astype(F32), gain)
        normed[0, at, :] = y.astype(BF16)
        for j in range(tangents):
            t = state[pl.ds((1 + j) * rows0 + b * toks, toks), :].astype(F32)
            normed[1 + j, at, :] = norm_tangent(t, centred, inverse, gain).astype(BF16)


def last_attend(sizes, u, normed):
    micro, toks, width, hd, tangents = sizes
    factor = HEAD ** (-0.5)
    shape = (u.shape[0], micro * toks)
    stream = stream_of(sizes, shape)
    image = (lax.broadcasted_iota(jnp.int32, shape, 0) % group_of(sizes)) % micro
    valid = lax.broadcasted_iota(jnp.int32, shape, 1) // toks == image
    parts = [dot_t(u, normed[s]) * factor for s in range(1 + tangents)]
    probs = softmax(jnp.where(valid, parts[0], -jnp.inf))
    weights = primal_rows(sizes, probs)
    scores = lowered(sizes, parts)
    dprobs = weights * (scores - jnp.sum(weights * scores, -1, keepdims=True))
    zero = jnp.zeros_like(weights)
    total = dot(jnp.where(stream == 0, weights, dprobs).astype(BF16), normed[0])
    for j in range(tangents):
        total = total + dot(jnp.where(stream == 1 + j, weights, zero).astype(BF16), normed[1 + j])
    return total.astype(BF16)


TOK, LA, LB, ATT, CLS, U, M, O1, O0, GAIN, STAGES = range(11)


def kernel(
    n, sizes, tokens, w_qkv, tangent_value, w_out, t_out, gain_in, final_in, head_in, mean_ref, var_ref,
    a_stage, b_stage, a0, a1, b1, b_full, tok, normed_all, acc, att_out, att_in, state, normed,
    gains, final_gain, head, cls_out, cls_all, u_out, u_all, m_out, m_all, o_out, o_all, classes,
    loads, a_out, a_send, a_recv, stage_send, stage_recv, far_send, far_recv, b_send, b_recv,
):
    micro, toks, width, hd, tangents = sizes
    streams = 1 + tangents
    part = hd // 4
    share = part // HEAD
    g = Place(n)
    me, section, place, z, nz = g.me, g.section, g.place, g.z, g.nz
    other = 1 - section
    rows = width // n
    slab = 4 * rows
    group = group_of(sizes)
    own = at_rows(me, rows)

    barrier = pltpu.get_barrier_semaphore()

    def greet(target, sec):
        pl.semaphore_signal(
            barrier, inc=1, device_id={"section": sec, "dp": target}, device_id_type=MESH
        )

    for k in range(1, nz):
        greet(((z + k) % nz) * 4 + place, section)
    for near in (g.diagonal, g.x_near, g.y_near):
        greet(near, section)
        greet(near, other)
    greet(me, other)

    def column(p):
        return pl.ds(p * part, part) if isinstance(p, int) else at_rows(p, part)

    def load(i, src, dst):
        return pltpu.make_async_copy(src, dst, loads.at[i])

    def stage_loads():
        moves = []
        for p in range(4):
            for m in range(3):
                moves.append((w_qkv.at[:, pl.ds(m * hd + p * part, part)], a_stage.at[p, :, pl.ds(m * part, part)]))
            for j in range(tangents):
                moves.append(
                    (
                        tangent_value.at[j, :, pl.ds(p * part, part)],
                        a_stage.at[p, :, pl.ds((3 + j) * part, part)],
                    )
                )
        return [load(8 + i, *move) for i, move in enumerate(moves)]

    def own_loads():
        moves = []
        for m in range(3):
            moves.append((w_qkv.at[:, column(m * 4 + place)], a1.at[own, pl.ds(m * part, part)]))
        for j in range(tangents):
            moves.append((tangent_value.at[j, :, column(place)], a1.at[own, pl.ds((3 + j) * part, part)]))
        moves.append((w_out.at[:, column(place)], b1.at[0, own, :]))
        moves.append((t_out.at[:, :, column(place)], b1.at[pl.ds(1, tangents), own, :]))
        for p in range(4):
            moves.append((w_out.at[:, pl.ds(p * part, part)], b_stage.at[p, 0]))
            moves.append((t_out.at[:, :, pl.ds(p * part, part)], b_stage.at[p, pl.ds(1, tangents)]))
        return [load(8 + 4 * (3 + tangents) + i, *move) for i, move in enumerate(moves)]

    def b_loads():
        return [
            load(4, w_out, b_full.at[0, own, :]),
            load(5, t_out, b_full.at[pl.ds(1, tangents), own, :]),
        ]

    def start_all(moves):
        for move in moves:
            move.start()

    def wait_all(moves):
        for move in moves:
            move.wait()

    def gain_load():
        return load(0, gain_in, gains.at[section])

    def tok_load():
        return load(1, tokens, tok.at[place])

    def tail_loads():
        return [load(2, head_in, head), load(3, final_in, final_gain)]

    start_all(stage_loads() + [gain_load(), tok_load()])
    pl.when(section == 0)(lambda: start_all(b_loads()))
    pl.when(section == 1)(lambda: start_all(own_loads()))
    start_all(tail_loads())
    pl.semaphore_wait(barrier, 7 + nz - 1)

    def xfer(stage, i, src, dst, source, target, sec):
        return pltpu.make_async_remote_copy(
            src_ref=src,
            dst_ref=dst,
            send_sem=stage_send.at[stage, i],
            recv_sem=stage_recv.at[stage, source],
            device_id={"section": sec, "dp": target},
            device_id_type=MESH,
        )

    def arrived(stage, source, dst):
        xfer(stage, 0, dst, dst, source, me, other).wait_recv()

    FAR = (3, 1, 2, 0)

    def scatter(stage, src, dst, sec, skip_own=False):
        sends = []
        for i in FAR:
            if i == 0 and skip_own:
                continue
            target = g.plane[i]
            move = xfer(stage, i, src(target % 4), dst, place, target, sec)
            move.start()
            sends.append(move)
        return sends

    def drain(sends):
        for move in sends:
            move.wait_send()

    def a_ref(src):
        return a0.at[at_rows(src, rows), :]

    def a_copy(src_ref, src, sem, target, sec):
        return pltpu.make_async_remote_copy(
            src_ref=src_ref,
            dst_ref=a_ref(src),
            send_sem=sem,
            recv_sem=a_recv.at[src],
            device_id={"section": sec, "dp": target},
            device_id_type=MESH,
        )

    @pl.when(section == 0)
    def _():
        sends = []
        wait_all(stage_loads())
        for i in (0, 3, 1, 2):
            target = g.plane[i]
            move = a_copy(a_stage.at[target % 4], me, a_out.at[i], target, other)
            move.start()
            sends.append(move)
        gain_load().wait()
        move = xfer(GAIN, 0, gains.at[section], gains.at[section], 0, me, other)
        move.start()
        sends.append(move)
        wait_all(b_loads())
        gather = Gather(n, g, b_full, b_send, b_recv)
        lag = 2
        for d in range(nz + lag):
            if d < nz:
                gather.direct(d)
            if d >= lag:
                gather.relay(d - lag)
        tok_load().wait()
        gather.rest()
        for p in range(4):
            arrived(ATT, p, att_in.at[:, pl.ds(p * part, part)])
        first_out(sizes, tok, place, b_full, att_in, state)
        cls_out[...] = class_rows(sizes, state)
        sends += scatter(CLS, lambda p: cls_out, cls_all.at[place], other)
        arrived(GAIN, 0, gains.at[other])
        last_norm(sizes, gains[1], state, normed)
        for p in range(4):
            arrived(U, p, u_all.at[p])
        u = jnp.concatenate([u_all[p] for p in range(4)], 0)
        m = last_attend(sizes, u, normed)
        for p in range(4):
            m_out[p] = m[p * share * group : (p + 1) * share * group]
        sends += scatter(M, lambda p: m_out.at[p], m_all.at[place], other)
        classes[...] = cls_out[...]
        for p in range(4):
            arrived(O0, p, o_all.at[p])
        drain(sends)
        gather.drain()

    @pl.when(section == 1)
    def _():
        sends = []
        gain_load().wait()
        move = xfer(GAIN, 0, gains.at[section], gains.at[section], 0, me, other)
        move.start()
        sends.append(move)
        tok_load().wait()
        sends += scatter(TOK, lambda p: tok.at[place], tok.at[place], section, True)

        a_sends = []

        def relay(d):
            for shift, cond in g.sources(d):

                def step(shift=shift, d=d):
                    for near in g.plane:
                        src = near + 4 * shift
                        a_copy(a_ref(src), src, a_send.at[src, 0], me, section).wait_recv()
                        if shift <= 0 and d < nz - 1:
                            pl.when(g.up)(
                                lambda: a_copy(a_ref(src), src, a_send.at[src, 0], me + 4, section).start()
                            )
                        if shift >= 0 and d < nz - 1:
                            pl.when(g.down)(
                                lambda: a_copy(a_ref(src), src, a_send.at[src, 1], me - 4, section).start()
                            )

                step() if cond is None else pl.when(cond)(step)

        def relay_end(d):
            for shift, cond in g.sources(d):

                def step(shift=shift):
                    for near in g.plane:
                        src = near + 4 * shift
                        if shift <= 0:
                            pl.when(g.up)(
                                lambda: a_copy(a_ref(src), src, a_send.at[src, 0], me + 4, section).wait_send()
                            )
                        if shift >= 0:
                            pl.when(g.down)(
                                lambda: a_copy(a_ref(src), src, a_send.at[src, 1], me - 4, section).wait_send()
                            )

                step() if cond is None else pl.when(cond)(step)

        def project(d):
            for shift, cond in g.sources(d):

                def step(shift=shift):
                    at = at_rows(z + shift, slab)
                    term = dot(normed_all[:, at], a0[at, :])
                    acc[...] = term if d == 0 else acc[...] + term

                step() if cond is None else pl.when(cond)(step)

        relay(0)
        wait_all(stage_loads())
        wait_all(own_loads())
        sends += scatter(LA, lambda p: a_stage.at[p], a1.at[own, :], section, True)
        sends += scatter(LB, lambda p: b_stage.at[p], b1.at[:, own, :], section, True)
        arrived(GAIN, 0, gains.at[other])
        first_norm(sizes, tok, gains[0], normed_all, place)
        relay(1)
        for near in g.plane[1:]:
            arrived(TOK, near % 4, tok.at[near % 4])
            first_norm(sizes, tok, gains[0], normed_all, near % 4)
        for d in range(2, nz):
            relay(d)
            project(d - 2)
        for d in range(max(nz - 2, 0), nz):
            project(d)

        def far(kind, zc):
            at = at_rows(zc, slab)
            if kind == 0:
                return a1.at[at, pl.ds(0, 2 * part)]
            if kind == 1:
                return a1.at[at, pl.ds(2 * part, streams * part)]
            return b1.at[:, at, :]

        def far_copy(kind, zc, slot, target):
            return pltpu.make_async_remote_copy(
                src_ref=far(kind, zc),
                dst_ref=far(kind, zc),
                send_sem=far_send.at[kind, slot],
                recv_sem=far_recv.at[kind, zc],
                device_id={"section": section, "dp": target},
                device_id_type=MESH,
            )

        def far_each(act):
            for k in range(1, nz):
                pl.when(z + k < nz)(functools.partial(act, k, 2 * k))
                pl.when(z >= k)(functools.partial(act, -k, 2 * k + 1))

        def far_start(kind):
            far_each(lambda k, slot: far_copy(kind, z, slot, me + 4 * k).start())

        def far_wait(kind):
            far_each(lambda k, slot: far_copy(kind, z + k, 0, me).wait_recv())

        def far_end(kind):
            far_each(lambda k, slot: far_copy(kind, z, slot, me + 4 * k).wait_send())

        for near in g.plane[1:]:
            arrived(LA, near % 4, a1.at[at_rows(near, rows), :])
            arrived(LB, near % 4, b1.at[:, at_rows(near, rows), :])
        for kind in range(3):
            far_start(kind)

        for turn in (FAR[:2], FAR[2:]):
            for i in turn:
                for b in range(micro):
                    first_attend(sizes, acc, att_out, g.plane[i] % 4, b)
            for i in turn:
                target = g.plane[i]
                move = xfer(ATT, i, att_out.at[target % 4], att_in.at[:, column(place)], place, target, other)
                move.start()
                sends.append(move)

        far_wait(0)
        for p in range(4):
            arrived(CLS, p, cls_all.at[p])
        x = jnp.concatenate([cls_all[p] for p in range(4)], 0)
        q = dot(norm_group(sizes, x, gains[1]), a1[:, pl.ds(0, part)]).astype(BF16).astype(F32)
        owner = lax.broadcasted_iota(jnp.int32, (group, part), 1) // HEAD
        zero = jnp.zeros((group, part), F32)
        spread = [
            jnp.where(owner == h, q[p * group : (p + 1) * group], zero) for p in range(4) for h in range(share)
        ]
        u = dot_t(jnp.concatenate(spread, 0).astype(BF16), a1[:, pl.ds(part, part)]).astype(BF16)
        tall = share * group
        for p in range(4):
            u_out[p] = u[p * tall : (p + 1) * tall]
        sends += scatter(U, lambda p: u_out.at[p], u_all.at[place], other)
        far_wait(1)
        for p in range(4):
            arrived(M, p, m_all.at[p])
        m = jnp.concatenate([m_all[p] for p in range(4)], 0)
        r = dot(m, a1[:, pl.ds(2 * part, streams * part)])
        mixed = lowered(sizes, [r[:, s * part : (s + 1) * part] for s in range(streams)])
        chosen = []
        for p in range(4):
            block = zero
            for h in range(share):
                at = p * tall + h * group
                block = jnp.where(owner == h, mixed[at : at + group], block)
            chosen.append(block)
        attended = jnp.concatenate(chosen, 0).astype(BF16)
        far_wait(2)
        out = lowered(sizes, [dot_t(attended, b1[s]) for s in range(streams)])
        for p in range(4):
            o_out[p] = out[p * group : (p + 1) * group]
        sends += scatter(O1, lambda p: o_out.at[p], o_all.at[place], section, True)
        sends += scatter(O0, lambda p: o_out.at[p], o_all.at[place], other)
        o_all[place] = o_out[place]
        classes[...] = cls_all[place]
        for near in g.plane[1:]:
            arrived(O1, near % 4, o_all.at[near % 4])
        drain(sends)
        for d in range(nz - 1):
            relay_end(d)
        for kind in range(3):
            far_end(kind)

    wait_all(tail_loads())
    total = o_all[0] + o_all[1] + o_all[2] + o_all[3]
    final = (classes[...] + total).astype(BF16).astype(F32)
    features = norm_group(sizes, final, final_gain[...])
    count = head.shape[0]
    cut = count // 16 * 16
    for at in [pl.ds(0, cut)] + [pl.ds(cut, count - cut)] * (cut < count):
        logits = dot_t(features, head[at, :])
        mean_ref[:, 0, at] = logits[:micro]
        var_ref[:, 0, at] = sum(
            logits[(1 + j) * micro : (2 + j) * micro] * logits[(1 + j) * micro : (2 + j) * micro]
            for j in range(tangents)
        )


def two_sections(n):
    def shards(tokens, w_qkv, w_output, tangent_value, tangent_output, layer_gain, final_gain, head):
        micro, _, toks, width = tokens.shape
        tangents = tangent_value.shape[1]
        hd = w_output.shape[1]
        count = head.shape[1]
        rows = width // n
        part = hd // 4
        nz = n // 4
        sizes = (micro, toks, width, hd, tangents)
        streams = 1 + tangents
        rows0 = micro * toks
        group = group_of(sizes)
        tall = part // HEAD * group
        vmem = pl.BlockSpec(memory_space=pltpu.VMEM)
        anywhere = pl.BlockSpec(memory_space=pl.ANY)
        dma = pltpu.SemaphoreType.DMA
        mean, var = pl.pallas_call(
            functools.partial(kernel, n, sizes),
            out_shape=[jax.ShapeDtypeStruct((micro, 1, count), F32)] * 2,
            in_specs=[anywhere] * 8,
            out_specs=[vmem, vmem],
            scratch_shapes=[
                pltpu.VMEM((4, rows, (2 + streams) * part), BF16),
                pltpu.VMEM((4, streams, rows, part), BF16),
                pltpu.VMEM((width, (2 + streams) * part), BF16),
                pltpu.VMEM((width, (2 + streams) * part), BF16),
                pltpu.VMEM((streams, width, part), BF16),
                pltpu.VMEM((streams, width, hd), BF16),
                pltpu.VMEM((4, rows0, width), BF16),
                pltpu.VMEM((4 * rows0, width), BF16),
                pltpu.VMEM((4 * rows0, (2 + streams) * part), F32),
                pltpu.VMEM((4, streams * rows0, part), BF16),
                pltpu.VMEM((streams * rows0, hd), BF16),
                pltpu.VMEM((streams * rows0, width), BF16),
                pltpu.VMEM((streams, rows0, width), BF16),
                pltpu.VMEM((2, 1, width), F32),
                pltpu.VMEM((1, width), F32),
                pltpu.VMEM((count, width), BF16),
                pltpu.VMEM((group, width), F32),
                pltpu.VMEM((4, group, width), F32),
                pltpu.VMEM((4, tall, width), BF16),
                pltpu.VMEM((4, tall, width), BF16),
                pltpu.VMEM((4, tall, width), BF16),
                pltpu.VMEM((4, tall, width), BF16),
                pltpu.VMEM((4, group, width), F32),
                pltpu.VMEM((4, group, width), F32),
                pltpu.VMEM((group, width), F32),
                dma((64,)),
                dma((4,)),
                dma((n, 2)),
                dma((n,)),
                dma((STAGES, 4)),
                dma((STAGES, 4)),
                dma((3, 2 * nz)),
                dma((3, nz)),
                dma((send_slots(n),)),
                dma((n, 2)),
            ],
            compiler_params=pltpu.CompilerParams(
                collective_id=0, has_side_effects=True, vmem_limit_bytes=60 * 2**20
            ),
        )(
            tokens.reshape(rows0, width),
            w_qkv[0],
            tangent_value[0],
            jnp.swapaxes(w_output[0], 0, 1),
            jnp.swapaxes(tangent_output[0], 1, 2),
            layer_gain,
            final_gain[None],
            head.T,
        )
        return mean, var

    return shards


def solution(mesh):
    n = mesh.shape["dp"]
    fast = mesh.shape["section"] == 2 and n % 4 == 0
    return jax.shard_map(
        two_sections(n) if fast else relay_shards,
        mesh=mesh,
        in_specs=(
            P(None, "dp", None, None),
            P("section", "dp", None),
            P("section", None, "dp"),
            P("section", None, "dp", None),
            P("section", None, None, "dp"),
            P("section", None),
            P(),
            P(None, "section"),
        ),
        out_specs=(P(None, "dp", "section"), P(None, "dp", "section")),
        check_vma=False,
    )
```

time: 77 us -> 61.5 us (0.80)
  Pallas kernels: 72.7 us -> 58.8 us
  other arithmetic: 1.59 us -> 0 us
    pallas_call x1, Pallas kernels: 72.7 us -> 58.8 us  [shards(): pl.pallas_call(functools.partial(kernel, n, sizes), out_shape=[jax.ShapeD...]
    transpose x1 -> x0, other arithmetic: 1.59 us -> none  [shards(): outs = jnp.swapaxes(jnp.concatenate([w_output, tangent_output[0]], 0), 1, 2)]
where the time goes in v1:
time: 61.5 us; the launch traced here: 61.4 us
  Pallas kernels  58.8 us (96%)
  local copies, waits for them, and re-layouts  1.86 us (3%)
  between operations  0.65 us (1%)
    pallas_call x1, Pallas kernels, shards(): pl.pallas_call(functools.partial(kernel, n, sizes), out_shape=[jax.ShapeD...  58.8 us
    unnamed x4, local copies, waits for them, and re-layouts  1.86 us

profile of v1, /device:TPU:0, one launch (start us, length us, event | category | flops | bytes accessed | tf_op | source)
XLA Modules:
  0.0 61.4 jit_solution(4853721184808181240)
XLA Ops:
  0.6 58.8 %shard_map.95 = (f32[2,1,500]{2,1,0:T(1,128)}, f32[2,1,500]{2,1,0:T(1,128)}) custom-call(bf16[160,1024]{1,0:T(8,128)(2,1)} %bitcast.12, bf16[64,1536]{1,0:T(8,128)(2,1)} %bitcast.13, bf16[2,64,512]{2,1,0:T(8,128)(2,1)} %bitcast.14, bf16[64,512]{1,0:T(8,128)(2,1)} %bitcast.16, bf16[2,64,512]{2,1,0:T(8,128)(2,1)} %bitcast.15, f32[1,1024]{1,0:T(1,128)} %gain_in.1, ...), custom_call_target="tpu_custom_call" | custom-call | tf_op jit(solution)/shard_map/pallas_call | solution.py:735
  59.5 0.0 copy-start
  59.5 1.3 %copy.12 = f32[2,1,500]{2,1,0:T(1,128)} copy(f32[2,1,500]{2,1,0:T(1,128)} %get-tuple-element.4) | data formatting | bytes 8000
  60.8 0.0 copy-done
  60.8 0.6 copy.13
Async XLA Ops:
  59.5 1.3 %copy-start = (f32[2,1,500]{2,1,0:T(1,128)S(1)}, f32[2,1,500]{2,1,0:T(1,128)}, u32[]{:S(2)}) copy-start(f32[2,1,500]{2,1,0:T(1,128)} %get-tuple-element.5) | copy-start | bytes 12004

commit v2 on v1

--- a/solution.py
+++ b/solution.py
@@ -117,60 +117,68 @@
         self.full, self.send, self.recv = full, send, recv
         self.rows = full.shape[1] // n
         self.g = g
-        self.sends = []
-        self.slot = 0
-
-    def copy(self, src, half, target, slot):
-        depth = self.rows // 2
-        at = pl.ds(pl.multiple_of(src * self.rows + half * depth, depth), depth)
-        ref = self.full.at[:, at, :]
+        self.ends = []
+
+    def span(self, start, count):
+        return self.full.at[:, pl.ds(pl.multiple_of(start, self.rows // 2), count), :]
+
+    def remote(self, ref, target, sem, recv):
         return pltpu.make_async_remote_copy(
             src_ref=ref,
             dst_ref=ref,
-            send_sem=self.send.at[slot],
-            recv_sem=self.recv.at[src, half],
+            send_sem=self.send.at[sem],
+            recv_sem=recv,
             device_id={"section": self.g.section, "dp": target},
             device_id_type=MESH,
         )
 
-    def forward(self, cond, src, half, target):
-        slot = self.slot
-        self.slot += 1
-
+    def copy(self, src, half, target, sem):
+        depth = self.rows // 2
+        ref = self.span(src * self.rows + half * depth, depth)
+        return self.remote(ref, target, sem, self.recv.at[src, half])
+
+    def forward(self, cond, src, half, target, sem):
         def go():
-            self.copy(src, half, target, slot).start()
-
+            self.copy(src, half, target, sem).start()
+
+        go() if cond is None else pl.when(cond)(go)
+
+    def ended(self, cond, pieces, sem):
         def end():
-            self.copy(src, half, target, slot).wait_send()
-
-        go() if cond is None else pl.when(cond)(go)
-        self.sends.append((cond, end))
+            self.remote(self.span(0, pieces * self.rows), self.g.me, sem, self.recv.at[0, 0]).wait_send()
+
+        self.ends.append((cond, end))
 
     def arrived(self, src, half):
         self.copy(src, half, self.g.me, 0).wait_recv()
 
     def direct(self, d):
         g = self.g
-        for shift, cond in g.sources(d):
+        for side, (shift, cond) in enumerate(g.sources(d)):
             src = g.me + 4 * shift
             for half in range(2):
                 if d > 0:
                     pl.when(cond)(functools.partial(self.arrived, src, half))
                 if shift <= 0 and d < self.nz - 1:
-                    self.forward(g.up if cond is None else cond & g.up, src, half, g.me + 4)
+                    self.forward(g.up if cond is None else cond & g.up, src, half, g.me + 4, 4 * d)
                 if shift >= 0 and d < self.nz - 1:
-                    self.forward(g.down if cond is None else cond & g.down, src, half, g.me - 4)
+                    self.forward(g.down if cond is None else cond & g.down, src, half, g.me - 4, 4 * d + 1)
                 for target in ((g.y_near, g.x_near), (g.x_near, g.y_near))[half]:
-                    self.forward(cond, src, half, target)
+                    self.forward(cond, src, half, target, 4 * d + 2 + side)
+            if shift <= 0 and d < self.nz - 1:
+                self.ended(g.up if cond is None else cond & g.up, 1, 4 * d)
+            if shift >= 0 and d < self.nz - 1:
+                self.ended(g.down if cond is None else cond & g.down, 1, 4 * d + 1)
+            self.ended(cond, 3, 4 * d + 2 + side)
 
     def relay(self, d):
         g = self.g
-        for shift, cond in g.sources(d):
+        for side, (shift, cond) in enumerate(g.sources(d)):
             for half, near, target in ((0, g.x_near, g.y_near), (1, g.y_near, g.x_near)):
                 src = near + 4 * shift
                 wait = functools.partial(self.arrived, src, half)
                 wait() if cond is None else pl.when(cond)(wait)
-                self.forward(cond, src, half, target)
+                self.forward(cond, src, half, target, 4 * d + 2 + side)
 
     def rest(self):
         g = self.g
@@ -182,13 +190,8 @@
             self.arrived(g.diagonal + up, 1)
 
     def drain(self):
-        for cond, end in self.sends:
+        for cond, end in self.ends:
             end() if cond is None else pl.when(cond)(end)
-
-
-def send_slots(n):
-    nz = n // 4
-    return 2 * (4 + 3 * 2 * (nz - 1) + 2 * nz)
 
 
 class Place:
@@ -350,14 +353,14 @@
     return total.astype(BF16)
 
 
-TOK, LA, LB, ATT, CLS, U, M, O1, O0, GAIN, STAGES = range(11)
+TOK, LA, LB, ATT, ATC, CLS, U, M, O1, O0, GAIN, FIRST, STAGES = range(13)
 
 
 def kernel(
-    n, sizes, tokens, w_qkv, tangent_value, w_out, t_out, gain_in, final_in, head_in, mean_ref, var_ref,
+    n, sizes, tokens, w_qkv, tangent_value, w_out, t_out, gain_in, final_in, head_in, logit_ref,
     a_stage, b_stage, a0, a1, b1, b_full, tok, normed_all, acc, att_out, att_in, state, normed,
-    gains, final_gain, head, cls_out, cls_all, u_out, u_all, m_out, m_all, o_out, o_all, classes,
-    loads, a_out, a_send, a_recv, stage_send, stage_recv, far_send, far_recv, b_send, b_recv,
+    gains, final_gain, head, atc_out, atc_all, atc_in, cls_out, cls_in, cls_all, u_out, u_all, m_out, m_all, o_out, o_all, classes,
+    loads, a_send, a_recv, stage_send, stage_recv, far_send, far_recv, b_send, b_recv,
 ):
     micro, toks, width, hd, tangents = sizes
     streams = 1 + tangents
@@ -392,45 +395,33 @@
         return pltpu.make_async_copy(src, dst, loads.at[i])
 
     def stage_loads():
-        moves = []
         for p in range(4):
             for m in range(3):
-                moves.append((w_qkv.at[:, pl.ds(m * hd + p * part, part)], a_stage.at[p, :, pl.ds(m * part, part)]))
+                load(5, w_qkv.at[:, pl.ds(m * hd + p * part, part)], a_stage.at[p, :, pl.ds(m * part, part)]).start()
             for j in range(tangents):
-                moves.append(
-                    (
-                        tangent_value.at[j, :, pl.ds(p * part, part)],
-                        a_stage.at[p, :, pl.ds((3 + j) * part, part)],
-                    )
-                )
-        return [load(8 + i, *move) for i, move in enumerate(moves)]
+                load(
+                    5,
+                    tangent_value.at[j, :, pl.ds(p * part, part)],
+                    a_stage.at[p, :, pl.ds((3 + j) * part, part)],
+                ).start()
 
     def own_loads():
-        moves = []
         for m in range(3):
-            moves.append((w_qkv.at[:, column(m * 4 + place)], a1.at[own, pl.ds(m * part, part)]))
+            load(6, w_qkv.at[:, column(m * 4 + place)], a1.at[own, pl.ds(m * part, part)]).start()
         for j in range(tangents):
-            moves.append((tangent_value.at[j, :, column(place)], a1.at[own, pl.ds((3 + j) * part, part)]))
-        moves.append((w_out.at[:, column(place)], b1.at[0, own, :]))
-        moves.append((t_out.at[:, :, column(place)], b1.at[pl.ds(1, tangents), own, :]))
+            load(6, tangent_value.at[j, :, column(place)], a1.at[own, pl.ds((3 + j) * part, part)]).start()
+        load(7, w_out.at[:, column(place)], b1.at[0, own, :]).start()
+        load(7, t_out.at[:, :, column(place)], b1.at[pl.ds(1, tangents), own, :]).start()
         for p in range(4):
-            moves.append((w_out.at[:, pl.ds(p * part, part)], b_stage.at[p, 0]))
-            moves.append((t_out.at[:, :, pl.ds(p * part, part)], b_stage.at[p, pl.ds(1, tangents)]))
-        return [load(8 + 4 * (3 + tangents) + i, *move) for i, move in enumerate(moves)]
+            load(8, w_out.at[:, pl.ds(p * part, part)], b_stage.at[p, 0]).start()
+            load(8, t_out.at[:, :, pl.ds(p * part, part)], b_stage.at[p, pl.ds(1, tangents)]).start()
 
     def b_loads():
-        return [
-            load(4, w_out, b_full.at[0, own, :]),
-            load(5, t_out, b_full.at[pl.ds(1, tangents), own, :]),
-        ]
-
-    def start_all(moves):
-        for move in moves:
-            move.start()
-
-    def wait_all(moves):
-        for move in moves:
-            move.wait()
+        load(4, w_out, b_full.at[0, own, :]).start()
+        load(4, t_out, b_full.at[pl.ds(1, tangents), own, :]).start()
+
+    def loaded(i, ref):
+        load(i, ref, ref).wait()
 
     def gain_load():
         return load(0, gain_in, gains.at[section])
@@ -441,41 +432,43 @@
     def tail_loads():
         return [load(2, head_in, head), load(3, final_in, final_gain)]
 
-    start_all(stage_loads() + [gain_load(), tok_load()])
-    pl.when(section == 0)(lambda: start_all(b_loads()))
-    pl.when(section == 1)(lambda: start_all(own_loads()))
-    start_all(tail_loads())
+    stage_loads()
+    gain_load().start()
+    tok_load().start()
+    pl.when(section == 0)(b_loads)
+    pl.when(section == 1)(own_loads)
+    for move in tail_loads():
+        move.start()
     pl.semaphore_wait(barrier, 7 + nz - 1)
 
-    def xfer(stage, i, src, dst, source, target, sec):
+    def xfer(stage, src, dst, target, sec):
         return pltpu.make_async_remote_copy(
             src_ref=src,
             dst_ref=dst,
-            send_sem=stage_send.at[stage, i],
-            recv_sem=stage_recv.at[stage, source],
+            send_sem=stage_send.at[stage],
+            recv_sem=stage_recv.at[stage],
             device_id={"section": sec, "dp": target},
             device_id_type=MESH,
         )
 
-    def arrived(stage, source, dst):
-        xfer(stage, 0, dst, dst, source, me, other).wait_recv()
+    def arrived(stage, ref):
+        xfer(stage, ref, ref, me, other).wait_recv()
+
+    sent = []
 
     FAR = (3, 1, 2, 0)
 
-    def scatter(stage, src, dst, sec, skip_own=False):
-        sends = []
+    def scatter(stage, src, dst, sec, total, skip_own=False):
         for i in FAR:
-            if i == 0 and skip_own:
-                continue
-            target = g.plane[i]
-            move = xfer(stage, i, src(target % 4), dst, place, target, sec)
-            move.start()
-            sends.append(move)
-        return sends
-
-    def drain(sends):
-        for move in sends:
-            move.wait_send()
+            if i > 0 or not skip_own:
+                target = g.plane[i]
+                xfer(stage, src(target % 4), dst, target, sec).start()
+        sent.append((stage, total))
+
+    def drain():
+        for stage, ref in sent:
+            xfer(stage, ref, ref, me, other).wait_send()
+        sent.clear()
 
     def a_ref(src):
         return a0.at[at_rows(src, rows), :]
@@ -492,18 +485,15 @@
 
     @pl.when(section == 0)
     def _():
-        sends = []
-        wait_all(stage_loads())
-        for i in (0, 3, 1, 2):
+        loaded(5, a_stage)
+        for i in range(4):
             target = g.plane[i]
-            move = a_copy(a_stage.at[target % 4], me, a_out.at[i], target, other)
-            move.start()
-            sends.append(move)
+            a_copy(a_stage.at[target % 4], me, stage_send.at[FIRST], target, other).start()
+        sent.append((FIRST, a_stage))
         gain_load().wait()
-        move = xfer(GAIN, 0, gains.at[section], gains.at[section], 0, me, other)
-        move.start()
-        sends.append(move)
-        wait_all(b_loads())
+        xfer(GAIN, gains.at[section], gains.at[section], me, other).start()
+        sent.append((GAIN, gains.at[section]))
+        loaded(4, b_full.at[:, own, :])
         gather = Gather(n, g, b_full, b_send, b_recv)
         lag = 2
         for d in range(nz + lag):
@@ -513,37 +503,32 @@
                 gather.relay(d - lag)
         tok_load().wait()
         gather.rest()
-        for p in range(4):
-            arrived(ATT, p, att_in.at[:, pl.ds(p * part, part)])
+        arrived(ATC, atc_in)
+        arrived(ATT, att_in)
+        cls_out[...] = lowered(sizes, [dot_t(atc_in[...], b_full[s]) for s in range(streams)])
+        xfer(CLS, cls_out, cls_in, me, other).start()
+        sent.append((CLS, cls_out))
         first_out(sizes, tok, place, b_full, att_in, state)
-        cls_out[...] = class_rows(sizes, state)
-        sends += scatter(CLS, lambda p: cls_out, cls_all.at[place], other)
-        arrived(GAIN, 0, gains.at[other])
+        arrived(GAIN, gains.at[other])
         last_norm(sizes, gains[1], state, normed)
-        for p in range(4):
-            arrived(U, p, u_all.at[p])
+        arrived(U, u_all)
         u = jnp.concatenate([u_all[p] for p in range(4)], 0)
         m = last_attend(sizes, u, normed)
         for p in range(4):
             m_out[p] = m[p * share * group : (p + 1) * share * group]
-        sends += scatter(M, lambda p: m_out.at[p], m_all.at[place], other)
-        classes[...] = cls_out[...]
-        for p in range(4):
-            arrived(O0, p, o_all.at[p])
-        drain(sends)
+        scatter(M, lambda p: m_out.at[p], m_all.at[place], other, m_out)
+        classes[...] = class_rows(sizes, state)
+        arrived(O0, o_all)
+        drain()
         gather.drain()
 
     @pl.when(section == 1)
     def _():
-        sends = []
         gain_load().wait()
-        move = xfer(GAIN, 0, gains.at[section], gains.at[section], 0, me, other)
-        move.start()
-        sends.append(move)
+        xfer(GAIN, gains.at[section], gains.at[section], me, other).start()
+        sent.append((GAIN, gains.at[section]))
         tok_load().wait()
-        sends += scatter(TOK, lambda p: tok.at[place], tok.at[place], section, True)
-
-        a_sends = []
+        scatter(TOK, lambda p: tok.at[place], tok.at[place], section, tok.at[pl.ds(0, 3)], True)
 
         def relay(d):
             for shift, cond in g.sources(d):
@@ -551,34 +536,36 @@
                 def step(shift=shift, d=d):
                     for near in g.plane:
                         src = near + 4 * shift
-                        a_copy(a_ref(src), src, a_send.at[src, 0], me, section).wait_recv()
+                        a_copy(a_ref(src), src, a_send.at[d, 0], me, section).wait_recv()
                         if shift <= 0 and d < nz - 1:
                             pl.when(g.up)(
-                                lambda: a_copy(a_ref(src), src, a_send.at[src, 0], me + 4, section).start()
+                                lambda: a_copy(a_ref(src), src, a_send.at[d, 0], me + 4, section).start()
                             )
                         if shift >= 0 and d < nz - 1:
                             pl.when(g.down)(
-                                lambda: a_copy(a_ref(src), src, a_send.at[src, 1], me - 4, section).start()
+                                lambda: a_copy(a_ref(src), src, a_send.at[d, 1], me - 4, section).start()
                             )
 
                 step() if cond is None else pl.when(cond)(step)
 
         def relay_end(d):
+            slab_ref = a0.at[pl.ds(0, slab), :]
             for shift, cond in g.sources(d):
 
-                def step(shift=shift):
-                    for near in g.plane:
-                        src = near + 4 * shift
-                        if shift <= 0:
-                            pl.when(g.up)(
-                                lambda: a_copy(a_ref(src), src, a_send.at[src, 0], me + 4, section).wait_send()
-                            )
-                        if shift >= 0:
-                            pl.when(g.down)(
-                                lambda: a_copy(a_ref(src), src, a_send.at[src, 1], me - 4, section).wait_send()
-                            )
-
-                step() if cond is None else pl.when(cond)(step)
+                def end(way):
+                    pltpu.make_async_remote_copy(
+                        src_ref=slab_ref,
+                        dst_ref=slab_ref,
+                        send_sem=a_send.at[d, way],
+                        recv_sem=a_recv.at[0],
+                        device_id={"section": section, "dp": me},
+                        device_id_type=MESH,
+                    ).wait_send()
+
+                if shift <= 0:
+                    pl.when(g.up if cond is None else cond & g.up)(functools.partial(end, 0))
+                if shift >= 0:
+                    pl.when(g.down if cond is None else cond & g.down)(functools.partial(end, 1))
 
         def project(d):
             for shift, cond in g.sources(d):
@@ -591,15 +578,17 @@
                 step() if cond is None else pl.when(cond)(step)
 
         relay(0)
-        wait_all(stage_loads())
-        wait_all(own_loads())
-        sends += scatter(LA, lambda p: a_stage.at[p], a1.at[own, :], section, True)
-        sends += scatter(LB, lambda p: b_stage.at[p], b1.at[:, own, :], section, True)
-        arrived(GAIN, 0, gains.at[other])
+        loaded(5, a_stage)
+        loaded(6, a1.at[own, :])
+        loaded(7, b1.at[:, own, :])
+        loaded(8, b_stage)
+        scatter(LA, lambda p: a_stage.at[p], a1.at[own, :], section, a_stage.at[pl.ds(0, 3)], True)
+        scatter(LB, lambda p: b_stage.at[p], b1.at[:, own, :], section, b_stage.at[pl.ds(0, 3)], True)
+        arrived(GAIN, gains.at[other])
         first_norm(sizes, tok, gains[0], normed_all, place)
         relay(1)
+        arrived(TOK, tok.at[pl.ds(0, 3)])
         for near in g.plane[1:]:
-            arrived(TOK, near % 4, tok.at[near % 4])
             first_norm(sizes, tok, gains[0], normed_all, near % 4)
         for d in range(2, nz):
             relay(d)
@@ -625,40 +614,82 @@
                 device_id_type=MESH,
             )
 
-        def far_each(act):
+        ends = (z == 0) | (z == nz - 1)
+
+        def far_sends(kind):
             for k in range(1, nz):
-                pl.when(z + k < nz)(functools.partial(act, k, 2 * k))
-                pl.when(z >= k)(functools.partial(act, -k, 2 * k + 1))
+                for way, slot in ((k, 2 * k), (-k, 2 * k + 1)):
+                    there = z + way
+                    when = (there >= 0) & (there < nz)
+                    if k > 1:
+                        when = when & (ends | ((there > 0) & (there < nz - 1)))
+                    yield when, functools.partial(far_copy, kind, z, slot, me + 4 * way)
+
+        def far_relay(kind):
+            for k in range(1, nz - 2):
+                yield (z == 1) & (z + k < nz - 1), z + k, functools.partial(far_copy, kind, z + k, 2 * nz + k, me - 4)
+                yield (z == nz - 2) & (z - k > 0), z - k, functools.partial(far_copy, kind, z - k, 3 * nz + k, me + 4)
 
         def far_start(kind):
-            far_each(lambda k, slot: far_copy(kind, z, slot, me + 4 * k).start())
+            for when, move in far_sends(kind):
+                pl.when(when)(lambda: move().start())
+
+        def far_pass(kind):
+            for when, zc, move in far_relay(kind):
+
+                def step():
+                    far_copy(kind, zc, 0, me).wait_recv()
+                    move().start()
+
+                pl.when(when)(step)
 
         def far_wait(kind):
-            far_each(lambda k, slot: far_copy(kind, z + k, 0, me).wait_recv())
+            for k in range(1, nz):
+                for way in (k, -k):
+                    there = z + way
+                    when = (there >= 0) & (there < nz)
+                    if 0 < k < nz - 2:
+                        passed = ((z == 1) & (there > 1) & (there < nz - 1)) | (
+                            (z == nz - 2) & (there > 0) & (there < nz - 2)
+                        )
+                        when = when & jnp.logical_not(passed)
+                    pl.when(when)(lambda: far_copy(kind, there, 0, me).wait_recv())
 
         def far_end(kind):
-            far_each(lambda k, slot: far_copy(kind, z, slot, me + 4 * k).wait_send())
-
-        for near in g.plane[1:]:
-            arrived(LA, near % 4, a1.at[at_rows(near, rows), :])
-            arrived(LB, near % 4, b1.at[:, at_rows(near, rows), :])
+            for when, move in far_sends(kind):
+                pl.when(when)(lambda: move().wait_send())
+            for when, zc, move in far_relay(kind):
+                pl.when(when)(lambda: move().wait_send())
+
+        arrived(LA, a1.at[pl.ds(0, 3 * rows), :])
+        arrived(LB, b1.at[:, pl.ds(0, 3 * rows), :])
         for kind in range(3):
             far_start(kind)
 
-        for turn in (FAR[:2], FAR[2:]):
-            for i in turn:
-                for b in range(micro):
-                    first_attend(sizes, acc, att_out, g.plane[i] % 4, b)
-            for i in turn:
-                target = g.plane[i]
-                move = xfer(ATT, i, att_out.at[target % 4], att_in.at[:, column(place)], place, target, other)
-                move.start()
-                sends.append(move)
-
+        for i in FAR:
+            for b in range(micro):
+                first_attend(sizes, acc, att_out, g.plane[i] % 4, b)
+            target = g.plane[i]
+            xfer(ATT, att_out.at[target % 4], att_in.at[:, column(place)], target, other).start()
+        sent.append((ATT, att_out))
+        firsts = []
+        for p in range(4):
+            for i in range(group):
+                at = pl.ds(i * toks, 16) if i < streams * micro else pl.ds(0, 16)
+                firsts.append(att_out[p, at, :].astype(F32)[:1])
+        atc_out[...] = jnp.concatenate(firsts, 0).astype(BF16)
+        scatter(ATC, lambda p: atc_out, atc_in.at[:, column(place)], other, atc_all)
+        far_pass(0)
+        fresh = []
+        blank = jnp.zeros((group - micro, width), F32)
+        for p in range(4):
+            fresh += [tok[p, pl.ds(b * toks, 16), :].astype(F32)[:1] for b in range(micro)] + [blank]
+        fresh = jnp.concatenate(fresh, 0)
         far_wait(0)
+        arrived(CLS, cls_in)
+        x = (fresh + cls_in[...]).astype(BF16).astype(F32)
         for p in range(4):
-            arrived(CLS, p, cls_all.at[p])
-        x = jnp.concatenate([cls_all[p] for p in range(4)], 0)
+            cls_all[p] = x[p * group : (p + 1) * group]
         q = dot(norm_group(sizes, x, gains[1]), a1[:, pl.ds(0, part)]).astype(BF16).astype(F32)
         owner = lax.broadcasted_iota(jnp.int32, (group, part), 1) // HEAD
         zero = jnp.zeros((group, part), F32)
@@ -669,10 +700,11 @@
         tall = share * group
         for p in range(4):
             u_out[p] = u[p * tall : (p + 1) * tall]
-        sends += scatter(U, lambda p: u_out.at[p], u_all.at[place], other)
+        scatter(U, lambda p: u_out.at[p], u_all.at[place], other, u_out)
+        far_pass(1)
+        far_pass(2)
         far_wait(1)
-        for p in range(4):
-            arrived(M, p, m_all.at[p])
+        arrived(M, m_all)
         m = jnp.concatenate([m_all[p] for p in range(4)], 0)
         r = dot(m, a1[:, pl.ds(2 * part, streams * part)])
         mixed = lowered(sizes, [r[:, s * part : (s + 1) * part] for s in range(streams)])
@@ -688,31 +720,25 @@
         out = lowered(sizes, [dot_t(attended, b1[s]) for s in range(streams)])
         for p in range(4):
             o_out[p] = out[p * group : (p + 1) * group]
-        sends += scatter(O1, lambda p: o_out.at[p], o_all.at[place], section, True)
-        sends += scatter(O0, lambda p: o_out.at[p], o_all.at[place], other)
+        scatter(O1, lambda p: o_out.at[p], o_all.at[place], section, o_out.at[pl.ds(0, 3)], True)
+        scatter(O0, lambda p: o_out.at[p], o_all.at[place], other, o_out)
         o_all[place] = o_out[place]
         classes[...] = cls_all[place]
-        for near in g.plane[1:]:
-            arrived(O1, near % 4, o_all.at[near % 4])
-        drain(sends)
+        arrived(O1, o_all.at[pl.ds(0, 3)])
+        drain()
         for d in range(nz - 1):
             relay_end(d)
         for kind in range(3):
             far_end(kind)
 
-    wait_all(tail_loads())
+    for move in tail_loads():
+        move.wait()
     total = o_all[0] + o_all[1] + o_all[2] + o_all[3]
     final = (classes[...] + total).astype(BF16).astype(F32)
     features = norm_group(sizes, final, final_gain[...])
-    count = head.shape[0]
-    cut = count // 16 * 16
-    for at in [pl.ds(0, cut)] + [pl.ds(cut, count - cut)] * (cut < count):
-        logits = dot_t(features, head[at, :])
-        mean_ref[:, 0, at] = logits[:micro]
-        var_ref[:, 0, at] = sum(
-            logits[(1 + j) * micro : (2 + j) * micro] * logits[(1 + j) * micro : (2 + j) * micro]
-            for j in range(tangents)
-        )
+    logits = dot_t(features, head[...])
+    for s in range(streams):
+        logit_ref[s, :, 0, :] = logits[s * micro : (s + 1) * micro]
 
 
 def two_sections(n):
@@ -732,11 +758,11 @@
         vmem = pl.BlockSpec(memory_space=pltpu.VMEM)
         anywhere = pl.BlockSpec(memory_space=pl.ANY)
         dma = pltpu.SemaphoreType.DMA
-        mean, var = pl.pallas_call(
+        logits = pl.pallas_call(
             functools.partial(kernel, n, sizes),
-            out_shape=[jax.ShapeDtypeStruct((micro, 1, count), F32)] * 2,
+            out_shape=jax.ShapeDtypeStruct((streams, micro, 1, count), F32),
             in_specs=[anywhere] * 8,
-            out_specs=[vmem, vmem],
+            out_specs=vmem,
             scratch_shapes=[
                 pltpu.VMEM((4, rows, (2 + streams) * part), BF16),
                 pltpu.VMEM((4, streams, rows, part), BF16),
@@ -754,7 +780,11 @@
                 pltpu.VMEM((2, 1, width), F32),
                 pltpu.VMEM((1, width), F32),
                 pltpu.VMEM((count, width), BF16),
-                pltpu.VMEM((group, width), F32),
+                pltpu.VMEM((4 * group, part), BF16),
+                pltpu.VMEM((16 * group, part), BF16),
+                pltpu.VMEM((4 * group, hd), BF16),
+                pltpu.VMEM((4 * group, width), F32),
+                pltpu.VMEM((4 * group, width), F32),
                 pltpu.VMEM((4, group, width), F32),
                 pltpu.VMEM((4, tall, width), BF16),
                 pltpu.VMEM((4, tall, width), BF16),
@@ -763,15 +793,14 @@
                 pltpu.VMEM((4, group, width), F32),
                 pltpu.VMEM((4, group, width), F32),
                 pltpu.VMEM((group, width), F32),
-                dma((64,)),
-                dma((4,)),
-                dma((n, 2)),
+                dma((9,)),
+                dma((nz, 2)),
                 dma((n,)),
-                dma((STAGES, 4)),
-                dma((STAGES, 4)),
-                dma((3, 2 * nz)),
+                dma((STAGES,)),
+                dma((STAGES,)),
+                dma((3, 4 * nz)),
                 dma((3, nz)),
-                dma((send_slots(n),)),
+                dma((4 * nz,)),
                 dma((n, 2)),
             ],
             compiler_params=pltpu.CompilerParams(
@@ -787,7 +816,7 @@
             final_gain[None],
             head.T,
         )
-        return mean, var
+        return logits[0], sum(logits[1 + j] * logits[1 + j] for j in range(tangents))
 
     return shards
 

time: 61.5 us -> 56 us (0.911)
  Pallas kernels: 58.8 us -> 53.9 us
  local copies, waits for them, and re-layouts: 1.86 us -> 0 us
  other arithmetic: 0 us -> 1.29 us
    pallas_call x1, Pallas kernels: 58.8 us -> 53.9 us  [shards(): pl.pallas_call(functools.partial(kernel, n, sizes), out_shape=jax.ShapeDt...]
    unnamed x4 -> x0, local copies, waits for them, and re-layouts: 1.86 us -> none
    add x0 -> x1, other arithmetic: none -> 1.29 us  [shards(): sum((logits[1 + j] * logits[1 + j] for j in range(tangents)))]
where the time goes in v2:
time: 56 us; the launch traced here: 55.8 us
  Pallas kernels  53.9 us (96%)
  other arithmetic  1.29 us (2%)
  between operations  0.64 us (1%)
    pallas_call x1, Pallas kernels, shards(): pl.pallas_call(functools.partial(kernel, n, sizes), out_shape=jax.ShapeDt...  53.9 us
    add x1, other arithmetic, shards(): sum((logits[1 + j] * logits[1 + j] for j in range(tangents)))  1.29 us

profile of v2, /device:TPU:0, one launch (start us, length us, event | category | flops | bytes accessed | tf_op | source)
XLA Modules:
  0.0 55.8 jit_solution(1281896217604617151)
XLA Ops:
  0.6 53.9 %shard_map.95 = f32[3,2,1,500]{3,2,1,0:T(1,128)} custom-call(bf16[160,1024]{1,0:T(8,128)(2,1)} %bitcast.16, bf16[64,1536]{1,0:T(8,128)(2,1)} %bitcast.17, bf16[2,64,512]{2,1,0:T(8,128)(2,1)} %bitcast.18, bf16[64,512]{1,0:T(8,128)(2,1)} %bitcast.20, bf16[2,64,512]{2,1,0:T(8,128)(2,1)} %bitcast.19, f32[1,1024]{1,0:T(1,128)} %gain_in.1, f32[1,1024]{1,0:T(1,128)} %bitcast.21, ...), custom_call_target="tpu_custom_call" | custom-call | tf_op jit(solution)/shard_map/pallas_call | solution.py:761
  54.5 1.3 %add_bitcast_fusion = (f32[2,1,500]{2,1,0:T(1,128)}, f32[2,1,500]{2,1,0:T(1,128)}) fusion(f32[3,2,1,500]{3,2,1,0:T(1,128)} %shard_map.95), kind=kLoop, calls=%fused_computation | loop fusion | flops 3000 | bytes 20000 | tf_op jit(solution)/shard_map/add | solution.py:819

commit v3 on v2

--- a/solution.py
+++ b/solution.py
@@ -152,24 +152,38 @@
     def arrived(self, src, half):
         self.copy(src, half, self.g.me, 0).wait_recv()
 
+    def along(self):
+        g, nz = self.g, self.nz
+        for k in range(1, nz):
+            for way in (k, -k):
+                when = g.reaches(way)
+                for half in range(2):
+                    self.forward(when, g.me, half, g.me + 4 * way, g.z + way)
+                self.ended(when, 1, g.z + way)
+
+    def pass_on(self, d):
+        g = self.g
+        for shift, cond in g.sources(d):
+            passed = g.passes(shift)
+            if passed is not None:
+                src = g.me + 4 * shift
+                for half in range(2):
+                    pl.when(passed)(functools.partial(self.arrived, src, half))
+                    self.forward(passed, src, half, g.me - 4 if shift > 0 else g.me + 4, self.nz + d)
+                self.ended(passed, 1, self.nz + d)
+
     def direct(self, d):
         g = self.g
         for side, (shift, cond) in enumerate(g.sources(d)):
             src = g.me + 4 * shift
+            passed = g.passes(shift)
             for half in range(2):
                 if d > 0:
-                    pl.when(cond)(functools.partial(self.arrived, src, half))
-                if shift <= 0 and d < self.nz - 1:
-                    self.forward(g.up if cond is None else cond & g.up, src, half, g.me + 4, 4 * d)
-                if shift >= 0 and d < self.nz - 1:
-                    self.forward(g.down if cond is None else cond & g.down, src, half, g.me - 4, 4 * d + 1)
+                    fresh = cond if passed is None else cond & jnp.logical_not(passed)
+                    pl.when(fresh)(functools.partial(self.arrived, src, half))
                 for target in ((g.y_near, g.x_near), (g.x_near, g.y_near))[half]:
-                    self.forward(cond, src, half, target, 4 * d + 2 + side)
-            if shift <= 0 and d < self.nz - 1:
-                self.ended(g.up if cond is None else cond & g.up, 1, 4 * d)
-            if shift >= 0 and d < self.nz - 1:
-                self.ended(g.down if cond is None else cond & g.down, 1, 4 * d + 1)
-            self.ended(cond, 3, 4 * d + 2 + side)
+                    self.forward(cond, src, half, target, 2 * self.nz + 2 * d + side)
+            self.ended(cond, 3, 2 * self.nz + 2 * d + side)
 
     def relay(self, d):
         g = self.g
@@ -178,7 +192,7 @@
                 src = near + 4 * shift
                 wait = functools.partial(self.arrived, src, half)
                 wait() if cond is None else pl.when(cond)(wait)
-                self.forward(cond, src, half, target, 4 * d + 2 + side)
+                self.forward(cond, src, half, target, 2 * self.nz + 2 * d + side)
 
     def rest(self):
         g = self.g
@@ -212,6 +226,20 @@
         if d == 0:
             return [(0, None)]
         return [(-d, self.z >= d), (d, self.z + d < self.nz)]
+
+    def reaches(self, way):
+        z, nz = self.z, self.nz
+        there = z + way
+        when = (there >= 0) & (there < nz)
+        if abs(way) > 1:
+            when = when & ((z == 0) | (z == nz - 1) | ((there > 0) & (there < nz - 1)))
+        return when
+
+    def passes(self, shift):
+        z, nz = self.z, self.nz
+        if not 0 < abs(shift) < nz - 2:
+            return None
+        return (z == 1) & (z + shift < nz - 1) if shift > 0 else (z == nz - 2) & (z + shift > 0)
 
 
 def norm_rows(x, gains):
@@ -353,7 +381,7 @@
     return total.astype(BF16)
 
 
-TOK, LA, LB, ATT, ATC, CLS, U, M, O1, O0, GAIN, FIRST, STAGES = range(13)
+TOK, TOKY, TOKD, LA, LB, ATT, ATC, CLS, U, M, O1, O0, GAIN, FIRST, STAGES = range(15)
 
 
 def kernel(
@@ -496,18 +524,20 @@
         loaded(4, b_full.at[:, own, :])
         gather = Gather(n, g, b_full, b_send, b_recv)
         lag = 2
+        gather.along()
         for d in range(nz + lag):
             if d < nz:
+                gather.pass_on(d)
                 gather.direct(d)
             if d >= lag:
                 gather.relay(d - lag)
         tok_load().wait()
         gather.rest()
         arrived(ATC, atc_in)
-        arrived(ATT, att_in)
         cls_out[...] = lowered(sizes, [dot_t(atc_in[...], b_full[s]) for s in range(streams)])
         xfer(CLS, cls_out, cls_in, me, other).start()
         sent.append((CLS, cls_out))
+        arrived(ATT, att_in)
         first_out(sizes, tok, place, b_full, att_in, state)
         arrived(GAIN, gains.at[other])
         last_norm(sizes, gains[1], state, normed)
@@ -528,13 +558,12 @@
         xfer(GAIN, gains.at[section], gains.at[section], me, other).start()
         sent.append((GAIN, gains.at[section]))
         tok_load().wait()
-        scatter(TOK, lambda p: tok.at[place], tok.at[place], section, tok.at[pl.ds(0, 3)], True)
-
-        def relay(d):
+
+        def relay(d, some=g.plane):
             for shift, cond in g.sources(d):
 
                 def step(shift=shift, d=d):
-                    for near in g.plane:
+                    for near in some:
                         src = near + 4 * shift
                         a_copy(a_ref(src), src, a_send.at[d, 0], me, section).wait_recv()
                         if shift <= 0 and d < nz - 1:
@@ -577,24 +606,26 @@
 
                 step() if cond is None else pl.when(cond)(step)
 
-        relay(0)
+        relay(0, g.plane[:1])
+        for stage, near in ((TOK, g.x_near), (TOKY, g.y_near)):
+            xfer(stage, tok.at[place], tok.at[place], near, section).start()
+            sent.append((stage, tok.at[place]))
         loaded(5, a_stage)
         loaded(6, a1.at[own, :])
         loaded(7, b1.at[:, own, :])
-        loaded(8, b_stage)
         scatter(LA, lambda p: a_stage.at[p], a1.at[own, :], section, a_stage.at[pl.ds(0, 3)], True)
-        scatter(LB, lambda p: b_stage.at[p], b1.at[:, own, :], section, b_stage.at[pl.ds(0, 3)], True)
+        relay(0, g.plane[1:])
         arrived(GAIN, gains.at[other])
         first_norm(sizes, tok, gains[0], normed_all, place)
         relay(1)
-        arrived(TOK, tok.at[pl.ds(0, 3)])
-        for near in g.plane[1:]:
-            first_norm(sizes, tok, gains[0], normed_all, near % 4)
-        for d in range(2, nz):
-            relay(d)
-            project(d - 2)
-        for d in range(max(nz - 2, 0), nz):
-            project(d)
+        half = micro * toks // 2
+        for stage, near, target, first in ((TOK, g.x_near, g.y_near, 0), (TOKY, g.y_near, g.x_near, half)):
+            arrived(stage, tok.at[near % 4])
+            piece = tok.at[near % 4, pl.ds(first, half), :]
+            xfer(TOKD, piece, piece, target, section).start()
+        sent.append((TOKD, tok.at[0]))
+        loaded(8, b_stage)
+        scatter(LB, lambda p: b_stage.at[p], b1.at[:, own, :], section, b_stage.at[pl.ds(0, 3)], True)
 
         def far(kind, zc):
             at = at_rows(zc, slab)
@@ -618,21 +649,22 @@
 
         def far_sends(kind):
             for k in range(1, nz):
-                for way, slot in ((k, 2 * k), (-k, 2 * k + 1)):
+                for way in (k, -k):
                     there = z + way
                     when = (there >= 0) & (there < nz)
                     if k > 1:
                         when = when & (ends | ((there > 0) & (there < nz - 1)))
-                    yield when, functools.partial(far_copy, kind, z, slot, me + 4 * way)
+                    yield when, functools.partial(far_copy, kind, z, there, me + 4 * way)
 
         def far_relay(kind):
             for k in range(1, nz - 2):
-                yield (z == 1) & (z + k < nz - 1), z + k, functools.partial(far_copy, kind, z + k, 2 * nz + k, me - 4)
-                yield (z == nz - 2) & (z - k > 0), z - k, functools.partial(far_copy, kind, z - k, 3 * nz + k, me + 4)
-
-        def far_start(kind):
-            for when, move in far_sends(kind):
-                pl.when(when)(lambda: move().start())
+                yield (z == 1) & (z + k < nz - 1), z + k, functools.partial(far_copy, kind, z + k, nz + k, me - 4)
+                yield (z == nz - 2) & (z - k > 0), z - k, functools.partial(far_copy, kind, z - k, nz + k, me + 4)
+
+        def far_start(kind, late):
+            for k, (when, move) in enumerate(far_sends(kind)):
+                if (k // 2 == nz - 2) == late:
+                    pl.when(when)(lambda: move().start())
 
         def far_pass(kind):
             for when, zc, move in far_relay(kind):
@@ -661,17 +693,38 @@
             for when, zc, move in far_relay(kind):
                 pl.when(when)(lambda: move().wait_send())
 
-        arrived(LA, a1.at[pl.ds(0, 3 * rows), :])
-        arrived(LB, b1.at[:, pl.ds(0, 3 * rows), :])
-        for kind in range(3):
-            far_start(kind)
+        def far_begin():
+            arrived(LA, a1.at[pl.ds(0, 3 * rows), :])
+            far_start(0, False)
+            far_start(1, False)
+
+        for near in (g.x_near, g.y_near):
+            first_norm(sizes, tok, gains[0], normed_all, near % 4)
+        for d in range(2, nz - 1):
+            relay(d)
+        arrived(TOKD, tok.at[g.diagonal % 4])
+        first_norm(sizes, tok, gains[0], normed_all, g.diagonal % 4)
+        for d in range(nz - 1):
+            project(d)
+        far_begin()
+        if nz > 2:
+            relay(nz - 1)
+        far_start(0, True)
+        far_start(1, True)
+        project(nz - 1)
+        def give(i):
+            target = g.plane[i]
+            xfer(ATT, att_out.at[target % 4], att_in.at[:, column(place)], target, other).start()
 
         for i in FAR:
             for b in range(micro):
                 first_attend(sizes, acc, att_out, g.plane[i] % 4, b)
-            target = g.plane[i]
-            xfer(ATT, att_out.at[target % 4], att_in.at[:, column(place)], target, other).start()
-        sent.append((ATT, att_out))
+            if i > 0:
+                give(i)
+            if i == FAR[1]:
+                arrived(LB, b1.at[:, pl.ds(0, 3 * rows), :])
+                far_start(2, False)
+                far_start(2, True)
         firsts = []
         for p in range(4):
             for i in range(group):
@@ -679,6 +732,8 @@
                 firsts.append(att_out[p, at, :].astype(F32)[:1])
         atc_out[...] = jnp.concatenate(firsts, 0).astype(BF16)
         scatter(ATC, lambda p: atc_out, atc_in.at[:, column(place)], other, atc_all)
+        give(0)
+        sent.append((ATT, att_out))
         far_pass(0)
         fresh = []
         blank = jnp.zeros((group - micro, width), F32)
@@ -719,7 +774,7 @@
         far_wait(2)
         out = lowered(sizes, [dot_t(attended, b1[s]) for s in range(streams)])
         for p in range(4):
-            o_out[p] = out[p * group : (p + 1) * group]
+            o_out[p] = out[p * group : (p + 1) * group].astype(BF16)
         scatter(O1, lambda p: o_out.at[p], o_all.at[place], section, o_out.at[pl.ds(0, 3)], True)
         scatter(O0, lambda p: o_out.at[p], o_all.at[place], other, o_out)
         o_all[place] = o_out[place]
@@ -733,7 +788,7 @@
 
     for move in tail_loads():
         move.wait()
-    total = o_all[0] + o_all[1] + o_all[2] + o_all[3]
+    total = sum(o_all[p].astype(F32) for p in range(4))
     final = (classes[...] + total).astype(BF16).astype(F32)
     features = norm_group(sizes, final, final_gain[...])
     logits = dot_t(features, head[...])
@@ -790,15 +845,15 @@
                 pltpu.VMEM((4, tall, width), BF16),
                 pltpu.VMEM((4, tall, width), BF16),
                 pltpu.VMEM((4, tall, width), BF16),
-                pltpu.VMEM((4, group, width), F32),
-                pltpu.VMEM((4, group, width), F32),
+                pltpu.VMEM((4, group, width), BF16),
+                pltpu.VMEM((4, group, width), BF16),
                 pltpu.VMEM((group, width), F32),
                 dma((9,)),
                 dma((nz, 2)),
                 dma((n,)),
                 dma((STAGES,)),
                 dma((STAGES,)),
-                dma((3, 4 * nz)),
+                dma((3, 2 * nz)),
                 dma((3, nz)),
                 dma((4 * nz,)),
                 dma((n, 2)),

time: 56 us -> 52.8 us (0.943)
  Pallas kernels: 53.9 us -> 50.7 us
    pallas_call x1, Pallas kernels: 53.9 us -> 50.7 us  [shards(): pl.pallas_call(functools.partial(kernel, n, sizes), out_shape=jax.ShapeDt...]
where the time goes in v3:
time: 52.8 us; the launch traced here: 52.6 us
  Pallas kernels  50.7 us (96%)
  other arithmetic  1.29 us (2%)
  between operations  0.64 us (1%)
    pallas_call x1, Pallas kernels, shards(): pl.pallas_call(functools.partial(kernel, n, sizes), out_shape=jax.ShapeDt...  50.7 us
    add x1, other arithmetic, shards(): sum((logits[1 + j] * logits[1 + j] for j in range(tangents)))  1.29 us

profile of v3, /device:TPU:0, one launch (start us, length us, event | category | flops | bytes accessed | tf_op | source)
XLA Modules:
  0.0 52.6 jit_solution(7713735931600743890)
XLA Ops:
  0.6 50.7 %shard_map.95 = f32[3,2,1,500]{3,2,1,0:T(1,128)} custom-call(bf16[160,1024]{1,0:T(8,128)(2,1)} %bitcast.16, bf16[64,1536]{1,0:T(8,128)(2,1)} %bitcast.17, bf16[2,64,512]{2,1,0:T(8,128)(2,1)} %bitcast.18, bf16[64,512]{1,0:T(8,128)(2,1)} %bitcast.20, bf16[2,64,512]{2,1,0:T(8,128)(2,1)} %bitcast.19, f32[1,1024]{1,0:T(1,128)} %gain_in.1, f32[1,1024]{1,0:T(1,128)} %bitcast.21, ...), custom_call_target="tpu_custom_call" | custom-call | tf_op jit(solution)/shard_map/pallas_call | solution.py:816
  51.3 1.3 %add_bitcast_fusion = (f32[2,1,500]{2,1,0:T(1,128)}, f32[2,1,500]{2,1,0:T(1,128)}) fusion(f32[3,2,1,500]{3,2,1,0:T(1,128)} %shard_map.95), kind=kLoop, calls=%fused_computation | loop fusion | flops 3000 | bytes 20000 | tf_op jit(solution)/shard_map/add | solution.py:874

commit v4 on v3

--- a/solution.py
+++ b/solution.py
@@ -152,9 +152,9 @@
     def arrived(self, src, half):
         self.copy(src, half, self.g.me, 0).wait_recv()
 
-    def along(self):
+    def along(self, far):
         g, nz = self.g, self.nz
-        for k in range(1, nz):
+        for k in range(2, nz) if far else range(1, min(nz, 2)):
             for way in (k, -k):
                 when = g.reaches(way)
                 for half in range(2):
@@ -283,11 +283,17 @@
     v = acc[rows, pl.ds(2 * part, streams * part)].astype(BF16)
     zero = jnp.zeros_like(q)
     both = jnp.concatenate([jnp.where(even, q, zero), jnp.where(even, zero, q)], 0).astype(BF16)
-    low = softmax(dot_t(both, k) * factor).astype(BF16)
-    out = dot(low, v)
+    scores = dot_t(both, k) * factor
+    low = jnp.exp(scores - jnp.max(scores, -1, keepdims=True)).astype(BF16)
+    out = dot(low, jnp.concatenate([v, jnp.ones((toks, part), BF16)], 1))
+
+    def joined(s):
+        at = slice(s * part, (s + 1) * part)
+        return jnp.where(even, out[:toks, at], out[toks:, at])
+
+    scale = 1.0 / joined(streams)
     for s in range(streams):
-        joined = jnp.where(even, out[:toks, s * part : (s + 1) * part], out[toks:, s * part : (s + 1) * part])
-        att[slot, pl.ds((s * micro + b) * toks, toks), :] = joined.astype(BF16)
+        att[slot, pl.ds((s * micro + b) * toks, toks), :] = (joined(s) * scale).astype(BF16)
 
 
 def first_out(sizes, tok, place, b_full, att, state):
@@ -381,14 +387,14 @@
     return total.astype(BF16)
 
 
-TOK, TOKY, TOKD, LA, LB, ATT, ATC, CLS, U, M, O1, O0, GAIN, FIRST, STAGES = range(15)
+TOK, TOKY, TOKD, LA, LB, ATT, ATC, CLS, U, M, O1, O0, GAIN, FIRST, EARLY, STAGES = range(16)
 
 
 def kernel(
     n, sizes, tokens, w_qkv, tangent_value, w_out, t_out, gain_in, final_in, head_in, logit_ref,
     a_stage, b_stage, a0, a1, b1, b_full, tok, normed_all, acc, att_out, att_in, state, normed,
     gains, final_gain, head, atc_out, atc_all, atc_in, cls_out, cls_in, cls_all, u_out, u_all, m_out, m_all, o_out, o_all, classes,
-    loads, a_send, a_recv, stage_send, stage_recv, far_send, far_recv, b_send, b_recv,
+    loads, line, a_send, a_recv, stage_send, stage_recv, far_send, far_recv, b_send, b_recv,
 ):
     micro, toks, width, hd, tangents = sizes
     streams = 1 + tangents
@@ -409,12 +415,20 @@
             barrier, inc=1, device_id={"section": sec, "dp": target}, device_id_type=MESH
         )
 
-    for k in range(1, nz):
-        greet(((z + k) % nz) * 4 + place, section)
+    pl.when(g.up)(lambda: greet(me + 4, section))
+    pl.when(g.down)(lambda: greet(me - 4, section))
     for near in (g.diagonal, g.x_near, g.y_near):
         greet(near, section)
         greet(near, other)
     greet(me, other)
+
+    def met():
+        if nz > 1:
+            middle = g.up & g.down
+            pl.when(middle)(lambda: pl.semaphore_wait(barrier, 9))
+            pl.when(jnp.logical_not(middle))(lambda: pl.semaphore_wait(barrier, 8))
+        else:
+            pl.semaphore_wait(barrier, 7)
 
     def column(p):
         return pl.ds(p * part, part) if isinstance(p, int) else at_rows(p, part)
@@ -467,7 +481,35 @@
     pl.when(section == 1)(own_loads)
     for move in tail_loads():
         move.start()
-    pl.semaphore_wait(barrier, 7 + nz - 1)
+    met()
+
+    def tell(way, level, target):
+        pl.semaphore_signal(
+            line.at[way, level], inc=1, device_id={"section": section, "dp": target}, device_id_type=MESH
+        )
+
+    if nz > 2:
+
+        @pl.when(g.up & g.down)
+        def _():
+            tell(0, 1, me + 4)
+            tell(1, 1, me - 4)
+
+    def far_met():
+        for level in range(1, nz - 1):
+
+            @pl.when(z - 1 - level >= 0)
+            def _():
+                pl.semaphore_wait(line.at[0, level], 1)
+                if level + 1 < nz - 1:
+                    pl.when(g.up)(lambda: tell(0, level + 1, me + 4))
+
+            @pl.when(z + 1 + level < nz)
+            def _():
+                pl.semaphore_wait(line.at[1, level], 1)
+                if level + 1 < nz - 1:
+                    pl.when(g.down)(lambda: tell(1, level + 1, me - 4))
+
 
     def xfer(stage, src, dst, target, sec):
         return pltpu.make_async_remote_copy(
@@ -524,11 +566,14 @@
         loaded(4, b_full.at[:, own, :])
         gather = Gather(n, g, b_full, b_send, b_recv)
         lag = 2
-        gather.along()
+        gather.along(False)
         for d in range(nz + lag):
             if d < nz:
                 gather.pass_on(d)
                 gather.direct(d)
+                if d == 0:
+                    far_met()
+                    gather.along(True)
             if d >= lag:
                 gather.relay(d - lag)
         tok_load().wait()
@@ -606,14 +651,32 @@
 
                 step() if cond is None else pl.when(cond)(step)
 
+        loaded(7, b1.at[:, own, :])
+        early = b1.at[:, pl.ds(0, (nz - 1) * rows), :]
+
+        def ahead(k):
+            for way in (k, -k):
+                there = (z + way >= 0) & (z + way < nz)
+
+                def go():
+                    xfer(EARLY, b1.at[:, own, :], b1.at[:, own, :], me + 4 * way, section).start()
+
+                pl.when(there)(go)
+
+        if nz > 1:
+            ahead(1)
+        if nz > 1:
+            sent.append((EARLY, early))
         relay(0, g.plane[:1])
         for stage, near in ((TOK, g.x_near), (TOKY, g.y_near)):
             xfer(stage, tok.at[place], tok.at[place], near, section).start()
             sent.append((stage, tok.at[place]))
         loaded(5, a_stage)
         loaded(6, a1.at[own, :])
-        loaded(7, b1.at[:, own, :])
         scatter(LA, lambda p: a_stage.at[p], a1.at[own, :], section, a_stage.at[pl.ds(0, 3)], True)
+        far_met()
+        for k in range(2, nz):
+            ahead(k)
         relay(0, g.plane[1:])
         arrived(GAIN, gains.at[other])
         first_norm(sizes, tok, gains[0], normed_all, place)
@@ -627,90 +690,87 @@
         loaded(8, b_stage)
         scatter(LB, lambda p: b_stage.at[p], b1.at[:, own, :], section, b_stage.at[pl.ds(0, 3)], True)
 
-        def far(kind, zc):
+        def far_refs(kind, zc):
             at = at_rows(zc, slab)
             if kind == 0:
-                return a1.at[at, pl.ds(0, 2 * part)]
+                return [a1.at[at, pl.ds(0, 2 * part)]]
             if kind == 1:
-                return a1.at[at, pl.ds(2 * part, streams * part)]
-            return b1.at[:, at, :]
-
-        def far_copy(kind, zc, slot, target):
+                return [a1.at[at, pl.ds(2 * part, streams * part)]]
+            return [b1.at[:, at_rows(near + 4 * (zc - z), rows), :] for near in g.plane[1:]]
+
+        def far_total(kind):
+            return far_refs(kind, 0)[0] if kind < 2 else b1.at[:, pl.ds(0, 3 * rows), :]
+
+        def far_copy(ref, kind, zc, slot, target):
             return pltpu.make_async_remote_copy(
-                src_ref=far(kind, zc),
-                dst_ref=far(kind, zc),
+                src_ref=ref,
+                dst_ref=ref,
                 send_sem=far_send.at[kind, slot],
                 recv_sem=far_recv.at[kind, zc],
                 device_id={"section": section, "dp": target},
                 device_id_type=MESH,
             )
 
-        ends = (z == 0) | (z == nz - 1)
-
-        def far_sends(kind):
+        def far_moves(kind):
             for k in range(1, nz):
                 for way in (k, -k):
                     there = z + way
-                    when = (there >= 0) & (there < nz)
-                    if k > 1:
-                        when = when & (ends | ((there > 0) & (there < nz - 1)))
-                    yield when, functools.partial(far_copy, kind, z, there, me + 4 * way)
-
-        def far_relay(kind):
-            for k in range(1, nz - 2):
-                yield (z == 1) & (z + k < nz - 1), z + k, functools.partial(far_copy, kind, z + k, nz + k, me - 4)
-                yield (z == nz - 2) & (z - k > 0), z - k, functools.partial(far_copy, kind, z - k, nz + k, me + 4)
-
-        def far_start(kind, late):
-            for k, (when, move) in enumerate(far_sends(kind)):
-                if (k // 2 == nz - 2) == late:
-                    pl.when(when)(lambda: move().start())
+                    when = (there >= 0) & (there < nz) if kind in (0,) else g.reaches(way)
+                    yield when, None, z, there, me + 4 * way
+            for k in () if kind in (0,) else range(1, nz - 2):
+                for way in (k, -k):
+                    yield g.passes(way), way, z + way, nz + k, me - 4 if way > 0 else me + 4
+
+        def far_start(kind):
+            for when, way, zc, slot, target in far_moves(kind):
+
+                def go():
+                    for ref in far_refs(kind, zc):
+                        far_copy(ref, kind, zc, slot, target).start()
+
+                if way is None:
+                    pl.when(when)(go)
 
         def far_pass(kind):
-            for when, zc, move in far_relay(kind):
+            for when, way, zc, slot, target in far_moves(kind):
 
                 def step():
-                    far_copy(kind, zc, 0, me).wait_recv()
-                    move().start()
-
-                pl.when(when)(step)
+                    far_copy(far_total(kind), kind, zc, 0, me).wait_recv()
+                    for ref in far_refs(kind, zc):
+                        far_copy(ref, kind, zc, slot, target).start()
+
+                if way is not None:
+                    pl.when(when)(step)
 
         def far_wait(kind):
             for k in range(1, nz):
                 for way in (k, -k):
                     there = z + way
                     when = (there >= 0) & (there < nz)
-                    if 0 < k < nz - 2:
-                        passed = ((z == 1) & (there > 1) & (there < nz - 1)) | (
-                            (z == nz - 2) & (there > 0) & (there < nz - 2)
-                        )
-                        when = when & jnp.logical_not(passed)
-                    pl.when(when)(lambda: far_copy(kind, there, 0, me).wait_recv())
+                    if kind not in (0,) and g.passes(way) is not None:
+                        when = when & jnp.logical_not(g.passes(way))
+                    pl.when(when)(lambda: far_copy(far_total(kind), kind, there, 0, me).wait_recv())
 
         def far_end(kind):
-            for when, move in far_sends(kind):
-                pl.when(when)(lambda: move().wait_send())
-            for when, zc, move in far_relay(kind):
-                pl.when(when)(lambda: move().wait_send())
+            for when, way, zc, slot, target in far_moves(kind):
+                pl.when(when)(lambda: far_copy(far_total(kind), kind, zc, slot, target).wait_send())
 
         def far_begin():
             arrived(LA, a1.at[pl.ds(0, 3 * rows), :])
-            far_start(0, False)
-            far_start(1, False)
+            far_start(0)
+            far_start(1)
 
         for near in (g.x_near, g.y_near):
             first_norm(sizes, tok, gains[0], normed_all, near % 4)
         for d in range(2, nz - 1):
             relay(d)
+        far_begin()
         arrived(TOKD, tok.at[g.diagonal % 4])
         first_norm(sizes, tok, gains[0], normed_all, g.diagonal % 4)
         for d in range(nz - 1):
             project(d)
-        far_begin()
         if nz > 2:
             relay(nz - 1)
-        far_start(0, True)
-        far_start(1, True)
         project(nz - 1)
         def give(i):
             target = g.plane[i]
@@ -719,12 +779,9 @@
         for i in FAR:
             for b in range(micro):
                 first_attend(sizes, acc, att_out, g.plane[i] % 4, b)
-            if i > 0:
-                give(i)
             if i == FAR[1]:
                 arrived(LB, b1.at[:, pl.ds(0, 3 * rows), :])
-                far_start(2, False)
-                far_start(2, True)
+                far_start(2)
         firsts = []
         for p in range(4):
             for i in range(group):
@@ -732,9 +789,9 @@
                 firsts.append(att_out[p, at, :].astype(F32)[:1])
         atc_out[...] = jnp.concatenate(firsts, 0).astype(BF16)
         scatter(ATC, lambda p: atc_out, atc_in.at[:, column(place)], other, atc_all)
-        give(0)
+        for i in FAR:
+            give(i)
         sent.append((ATT, att_out))
-        far_pass(0)
         fresh = []
         blank = jnp.zeros((group - micro, width), F32)
         for p in range(4):
@@ -772,6 +829,8 @@
             chosen.append(block)
         attended = jnp.concatenate(chosen, 0).astype(BF16)
         far_wait(2)
+        if nz > 1:
+            arrived(EARLY, early)
         out = lowered(sizes, [dot_t(attended, b1[s]) for s in range(streams)])
         for p in range(4):
             o_out[p] = out[p * group : (p + 1) * group].astype(BF16)
@@ -815,7 +874,7 @@
         dma = pltpu.SemaphoreType.DMA
         logits = pl.pallas_call(
             functools.partial(kernel, n, sizes),
-            out_shape=jax.ShapeDtypeStruct((streams, micro, 1, count), F32),
+            out_shape=pltpu.VMEM((streams, micro, 1, count), F32),
             in_specs=[anywhere] * 8,
             out_specs=vmem,
             scratch_shapes=[
@@ -849,6 +908,7 @@
                 pltpu.VMEM((4, group, width), BF16),
                 pltpu.VMEM((group, width), F32),
                 dma((9,)),
+                pltpu.SemaphoreType.REGULAR((2, max(nz - 1, 1))),
                 dma((nz, 2)),
                 dma((n,)),
                 dma((STAGES,)),
@@ -859,7 +919,7 @@
                 dma((n, 2)),
             ],
             compiler_params=pltpu.CompilerParams(
-                collective_id=0, has_side_effects=True, vmem_limit_bytes=60 * 2**20
+                collective_id=0, has_side_effects=True, vmem_limit_bytes=63 * 2**20
             ),
         )(
             tokens.reshape(rows0, width),

time: 52.8 us -> 50.5 us (0.956)
  Pallas kernels: 50.7 us -> 49.1 us
  other arithmetic: 1.29 us -> 0.6 us
    pallas_call x1, Pallas kernels: 50.7 us -> 49.1 us  [shards(): pl.pallas_call(functools.partial(kernel, n, sizes), out_shape=pltpu.VMEM(...]
    add x1, other arithmetic: 1.29 us -> 0.6 us  [shards(): sum((logits[1 + j] * logits[1 + j] for j in range(tangents)))]
where the time goes in v4:
time: 50.5 us; the launch traced here: 50.3 us
  Pallas kernels  49.1 us (97%)
  between operations  0.64 us (1%)
  other arithmetic  0.6 us (1%)
    pallas_call x1, Pallas kernels, shards(): pl.pallas_call(functools.partial(kernel, n, sizes), out_shape=pltpu.VMEM(...  49.1 us

profile of v4, /device:TPU:0, one launch (start us, length us, event | category | flops | bytes accessed | tf_op | source)
XLA Modules:
  0.0 50.3 jit_solution(836794104912036621)
XLA Ops:
  0.6 49.1 %shard_map.95 = f32[3,2,1,500]{3,2,1,0:T(1,128)S(1)} custom-call(bf16[160,1024]{1,0:T(8,128)(2,1)} %bitcast.16, bf16[64,1536]{1,0:T(8,128)(2,1)} %bitcast.17, bf16[2,64,512]{2,1,0:T(8,128)(2,1)} %bitcast.18, bf16[64,512]{1,0:T(8,128)(2,1)} %bitcast.20, bf16[2,64,512]{2,1,0:T(8,128)(2,1)} %bitcast.19, f32[1,1024]{1,0:T(1,128)} %gain_in.1, ...), custom_call_target="tpu_custom_call" | custom-call | tf_op jit(solution)/shard_map/pallas_call | solution.py:875
  49.7 0.6 %add_bitcast_fusion = (f32[2,1,500]{2,1,0:T(1,128)}, f32[2,1,500]{2,1,0:T(1,128)}) fusion(f32[3,2,1,500]{3,2,1,0:T(1,128)S(1)} %shard_map.95), kind=kLoop, calls=%fused_computation | loop fusion | flops 3000 | bytes 20000 | tf_op jit(solution)/shard_map/add | solution.py:934

commit v5 on v4

--- a/solution.py
+++ b/solution.py
@@ -605,22 +605,22 @@
         tok_load().wait()
 
         def relay(d, some=g.plane):
-            for shift, cond in g.sources(d):
-
-                def step(shift=shift, d=d):
-                    for near in some:
+            for near in some:
+                for shift, cond in g.sources(d)[::-1]:
+
+                    def step():
                         src = near + 4 * shift
                         a_copy(a_ref(src), src, a_send.at[d, 0], me, section).wait_recv()
+                        if shift >= 0 and d < nz - 1:
+                            pl.when(g.down)(
+                                lambda: a_copy(a_ref(src), src, a_send.at[d, 1], me - 4, section).start()
+                            )
                         if shift <= 0 and d < nz - 1:
                             pl.when(g.up)(
                                 lambda: a_copy(a_ref(src), src, a_send.at[d, 0], me + 4, section).start()
                             )
-                        if shift >= 0 and d < nz - 1:
-                            pl.when(g.down)(
-                                lambda: a_copy(a_ref(src), src, a_send.at[d, 1], me - 4, section).start()
-                            )
-
-                step() if cond is None else pl.when(cond)(step)
+
+                    step() if cond is None else pl.when(cond)(step)
 
         def relay_end(d):
             slab_ref = a0.at[pl.ds(0, slab), :]
@@ -715,9 +715,9 @@
             for k in range(1, nz):
                 for way in (k, -k):
                     there = z + way
-                    when = (there >= 0) & (there < nz) if kind in (0,) else g.reaches(way)
+                    when = (there >= 0) & (there < nz) if kind in () else g.reaches(way)
                     yield when, None, z, there, me + 4 * way
-            for k in () if kind in (0,) else range(1, nz - 2):
+            for k in () if kind in () else range(1, nz - 2):
                 for way in (k, -k):
                     yield g.passes(way), way, z + way, nz + k, me - 4 if way > 0 else me + 4
 
@@ -747,7 +747,7 @@
                 for way in (k, -k):
                     there = z + way
                     when = (there >= 0) & (there < nz)
-                    if kind not in (0,) and g.passes(way) is not None:
+                    if kind not in () and g.passes(way) is not None:
                         when = when & jnp.logical_not(g.passes(way))
                     pl.when(when)(lambda: far_copy(far_total(kind), kind, there, 0, me).wait_recv())
 
@@ -792,6 +792,7 @@
         for i in FAR:
             give(i)
         sent.append((ATT, att_out))
+        far_pass(0)
         fresh = []
         blank = jnp.zeros((group - micro, width), F32)
         for p in range(4):

time: 50.5 us -> 47.7 us (0.945)
  Pallas kernels: 49.1 us -> 46.3 us
    pallas_call x1, Pallas kernels: 49.1 us -> 46.3 us  [shards(): pl.pallas_call(functools.partial(kernel, n, sizes), out_shape=pltpu.VMEM(...]
where the time goes in v5:
time: 47.7 us; the launch traced here: 47.6 us
  Pallas kernels  46.3 us (97%)
  between operations  0.64 us (1%)
  other arithmetic  0.6 us (1%)
    pallas_call x1, Pallas kernels, shards(): pl.pallas_call(functools.partial(kernel, n, sizes), out_shape=pltpu.VMEM(...  46.3 us

profile of v5, /device:TPU:0, one launch (start us, length us, event | category | flops | bytes accessed | tf_op | source)
XLA Modules:
  0.0 47.6 jit_solution(4566983998974471347)
XLA Ops:
  0.6 46.3 %shard_map.95 = f32[3,2,1,500]{3,2,1,0:T(1,128)S(1)} custom-call(bf16[160,1024]{1,0:T(8,128)(2,1)} %bitcast.16, bf16[64,1536]{1,0:T(8,128)(2,1)} %bitcast.17, bf16[2,64,512]{2,1,0:T(8,128)(2,1)} %bitcast.18, bf16[64,512]{1,0:T(8,128)(2,1)} %bitcast.20, bf16[2,64,512]{2,1,0:T(8,128)(2,1)} %bitcast.19, f32[1,1024]{1,0:T(1,128)} %gain_in.1, ...), custom_call_target="tpu_custom_call" | custom-call | tf_op jit(solution)/shard_map/pallas_call | solution.py:876
  46.9 0.6 %add_bitcast_fusion = (f32[2,1,500]{2,1,0:T(1,128)}, f32[2,1,500]{2,1,0:T(1,128)}) fusion(f32[3,2,1,500]{3,2,1,0:T(1,128)S(1)} %shard_map.95), kind=kLoop, calls=%fused_computation | loop fusion | flops 3000 | bytes 20000 | tf_op jit(solution)/shard_map/add | solution.py:935

commit v6 on v5

--- a/solution.py
+++ b/solution.py
@@ -117,95 +117,86 @@
         self.full, self.send, self.recv = full, send, recv
         self.rows = full.shape[1] // n
         self.g = g
-        self.ends = []
-
-    def span(self, start, count):
-        return self.full.at[:, pl.ds(pl.multiple_of(start, self.rows // 2), count), :]
 
     def remote(self, ref, target, sem, recv):
         return pltpu.make_async_remote_copy(
             src_ref=ref,
             dst_ref=ref,
             send_sem=self.send.at[sem],
-            recv_sem=recv,
+            recv_sem=self.recv.at[recv],
             device_id={"section": self.g.section, "dp": target},
             device_id_type=MESH,
         )
 
-    def copy(self, src, half, target, sem):
+    def half(self, src, half):
         depth = self.rows // 2
-        ref = self.span(src * self.rows + half * depth, depth)
-        return self.remote(ref, target, sem, self.recv.at[src, half])
-
-    def forward(self, cond, src, half, target, sem):
+        return self.full.at[:, pl.ds(pl.multiple_of(src * self.rows + half * depth, depth), depth), :]
+
+    def total(self, pieces):
+        return self.full.at[:, pl.ds(0, pieces * self.rows), :]
+
+    def line(self, plane, half):
+        return 2 * plane + half
+
+    def turn(self, plane, way):
+        return 2 * self.nz + 2 * plane + way
+
+    def forward(self, cond, src, half, target, sem, recv):
         def go():
-            self.copy(src, half, target, sem).start()
+            self.remote(self.half(src, half), target, sem, recv).start()
 
         go() if cond is None else pl.when(cond)(go)
 
-    def ended(self, cond, pieces, sem):
-        def end():
-            self.remote(self.span(0, pieces * self.rows), self.g.me, sem, self.recv.at[0, 0]).wait_send()
-
-        self.ends.append((cond, end))
-
-    def arrived(self, src, half):
-        self.copy(src, half, self.g.me, 0).wait_recv()
+    def arrived(self, src, half, recv):
+        self.remote(self.half(src, half), self.g.me, 0, recv).wait_recv()
 
     def along(self, far):
         g, nz = self.g, self.nz
         for k in range(2, nz) if far else range(1, min(nz, 2)):
             for way in (k, -k):
-                when = g.reaches(way)
                 for half in range(2):
-                    self.forward(when, g.me, half, g.me + 4 * way, g.z + way)
-                self.ended(when, 1, g.z + way)
+                    self.forward(g.reaches(way), g.me, half, g.me + 4 * way, 0, self.line(g.z, half))
 
     def pass_on(self, d):
         g = self.g
         for shift, cond in g.sources(d):
             passed = g.passes(shift)
             if passed is not None:
-                src = g.me + 4 * shift
+                src, plane = g.me + 4 * shift, g.z + shift
                 for half in range(2):
-                    pl.when(passed)(functools.partial(self.arrived, src, half))
-                    self.forward(passed, src, half, g.me - 4 if shift > 0 else g.me + 4, self.nz + d)
-                self.ended(passed, 1, self.nz + d)
+                    pl.when(passed)(functools.partial(self.arrived, src, half, self.line(plane, half)))
+                    target = g.me - 4 if shift > 0 else g.me + 4
+                    self.forward(passed, src, half, target, 0, self.line(plane, half))
 
     def direct(self, d):
         g = self.g
-        for side, (shift, cond) in enumerate(g.sources(d)):
-            src = g.me + 4 * shift
+        for shift, cond in g.sources(d):
+            src, plane = g.me + 4 * shift, g.z + shift
             passed = g.passes(shift)
             for half in range(2):
                 if d > 0:
                     fresh = cond if passed is None else cond & jnp.logical_not(passed)
-                    pl.when(fresh)(functools.partial(self.arrived, src, half))
-                for target in ((g.y_near, g.x_near), (g.x_near, g.y_near))[half]:
-                    self.forward(cond, src, half, target, 2 * self.nz + 2 * d + side)
-            self.ended(cond, 3, 2 * self.nz + 2 * d + side)
+                    pl.when(fresh)(functools.partial(self.arrived, src, half, self.line(plane, half)))
+                for way in (1 - half, half):
+                    recv = self.turn(plane, way) if way == half else 4 * self.nz
+                    self.forward(cond, src, half, (g.x_near, g.y_near)[way], 1, recv)
 
     def relay(self, d):
         g = self.g
-        for side, (shift, cond) in enumerate(g.sources(d)):
-            for half, near, target in ((0, g.x_near, g.y_near), (1, g.y_near, g.x_near)):
+        for shift, cond in g.sources(d):
+            for way, near, target in ((0, g.x_near, g.y_near), (1, g.y_near, g.x_near)):
                 src = near + 4 * shift
-                wait = functools.partial(self.arrived, src, half)
+                wait = functools.partial(self.arrived, src, way, self.turn(g.z + shift, way))
                 wait() if cond is None else pl.when(cond)(wait)
-                self.forward(cond, src, half, target, 2 * self.nz + 2 * d + side)
+                self.forward(cond, src, way, target, 1, 4 * self.nz)
 
     def rest(self):
-        g = self.g
-        for z in range(self.nz):
-            up = 4 * (z - g.z)
-            self.arrived(g.x_near + up, 1)
-            self.arrived(g.y_near + up, 0)
-            self.arrived(g.diagonal + up, 0)
-            self.arrived(g.diagonal + up, 1)
+        self.remote(self.total(2 * self.nz), self.g.me, 0, 4 * self.nz).wait_recv()
 
     def drain(self):
-        for cond, end in self.ends:
-            end() if cond is None else pl.when(cond)(end)
+        if self.nz > 1:
+            self.remote(self.total(self.nz - 1), self.g.me, 0, 0).wait_send()
+        self.remote(self.total(3 * self.nz), self.g.me, 1, 0).wait_send()
 
 
 class Place:
@@ -593,9 +584,9 @@
             m_out[p] = m[p * share * group : (p + 1) * share * group]
         scatter(M, lambda p: m_out.at[p], m_all.at[place], other, m_out)
         classes[...] = class_rows(sizes, state)
+        gather.drain()
+        drain()
         arrived(O0, o_all)
-        drain()
-        gather.drain()
 
     @pl.when(section == 1)
     def _():
@@ -701,11 +692,11 @@
         def far_total(kind):
             return far_refs(kind, 0)[0] if kind < 2 else b1.at[:, pl.ds(0, 3 * rows), :]
 
-        def far_copy(ref, kind, zc, slot, target):
+        def far_copy(ref, kind, zc, target):
             return pltpu.make_async_remote_copy(
                 src_ref=ref,
                 dst_ref=ref,
-                send_sem=far_send.at[kind, slot],
+                send_sem=far_send.at[kind],
                 recv_sem=far_recv.at[kind, zc],
                 device_id={"section": section, "dp": target},
                 device_id_type=MESH,
@@ -714,30 +705,28 @@
         def far_moves(kind):
             for k in range(1, nz):
                 for way in (k, -k):
-                    there = z + way
-                    when = (there >= 0) & (there < nz) if kind in () else g.reaches(way)
-                    yield when, None, z, there, me + 4 * way
-            for k in () if kind in () else range(1, nz - 2):
+                    yield g.reaches(way), None, z, me + 4 * way
+            for k in range(1, nz - 2):
                 for way in (k, -k):
-                    yield g.passes(way), way, z + way, nz + k, me - 4 if way > 0 else me + 4
+                    yield g.passes(way), way, z + way, me - 4 if way > 0 else me + 4
 
         def far_start(kind):
-            for when, way, zc, slot, target in far_moves(kind):
+            for when, way, zc, target in far_moves(kind):
 
                 def go():
                     for ref in far_refs(kind, zc):
-                        far_copy(ref, kind, zc, slot, target).start()
+                        far_copy(ref, kind, zc, target).start()
 
                 if way is None:
                     pl.when(when)(go)
 
         def far_pass(kind):
-            for when, way, zc, slot, target in far_moves(kind):
+            for when, way, zc, target in far_moves(kind):
 
                 def step():
-                    far_copy(far_total(kind), kind, zc, 0, me).wait_recv()
+                    far_copy(far_total(kind), kind, zc, me).wait_recv()
                     for ref in far_refs(kind, zc):
-                        far_copy(ref, kind, zc, slot, target).start()
+                        far_copy(ref, kind, zc, target).start()
 
                 if way is not None:
                     pl.when(when)(step)
@@ -747,13 +736,19 @@
                 for way in (k, -k):
                     there = z + way
                     when = (there >= 0) & (there < nz)
-                    if kind not in () and g.passes(way) is not None:
+                    if g.passes(way) is not None:
                         when = when & jnp.logical_not(g.passes(way))
-                    pl.when(when)(lambda: far_copy(far_total(kind), kind, there, 0, me).wait_recv())
+                    pl.when(when)(lambda: far_copy(far_total(kind), kind, there, me).wait_recv())
 
         def far_end(kind):
-            for when, way, zc, slot, target in far_moves(kind):
-                pl.when(when)(lambda: far_copy(far_total(kind), kind, zc, slot, target).wait_send())
+            count = nz - 1
+            if kind < 2:
+                first, last = ((0, 2), (2, 2 + streams))[kind]
+                ref = a1.at[pl.ds(0, count * slab), pl.ds(first * part, (last - first) * part)]
+            else:
+                ref = b1.at[:, pl.ds(0, count * 3 * rows), :]
+            if count > 0:
+                far_copy(ref, kind, 0, me).wait_send()
 
         def far_begin():
             arrived(LA, a1.at[pl.ds(0, 3 * rows), :])
@@ -835,16 +830,16 @@
         out = lowered(sizes, [dot_t(attended, b1[s]) for s in range(streams)])
         for p in range(4):
             o_out[p] = out[p * group : (p + 1) * group].astype(BF16)
+        scatter(O0, lambda p: o_out.at[p], o_all.at[place], other, o_out)
         scatter(O1, lambda p: o_out.at[p], o_all.at[place], section, o_out.at[pl.ds(0, 3)], True)
-        scatter(O0, lambda p: o_out.at[p], o_all.at[place], other, o_out)
         o_all[place] = o_out[place]
         classes[...] = cls_all[place]
-        arrived(O1, o_all.at[pl.ds(0, 3)])
-        drain()
         for d in range(nz - 1):
             relay_end(d)
         for kind in range(3):
             far_end(kind)
+        drain()
+        arrived(O1, o_all.at[pl.ds(0, 3)])
 
     for move in tail_loads():
         move.wait()
@@ -914,10 +909,10 @@
                 dma((n,)),
                 dma((STAGES,)),
                 dma((STAGES,)),
-                dma((3, 2 * nz)),
+                dma((3,)),
                 dma((3, nz)),
-                dma((4 * nz,)),
-                dma((n, 2)),
+                dma((2,)),
+                dma((4 * nz + 1,)),
             ],
             compiler_params=pltpu.CompilerParams(
                 collective_id=0, has_side_effects=True, vmem_limit_bytes=63 * 2**20
@@ -939,7 +934,7 @@
 
 def solution(mesh):
     n = mesh.shape["dp"]
-    fast = mesh.shape["section"] == 2 and n % 4 == 0
+    fast = mesh.shape["section"] == 2 and n % 4 == 0 and n // 4 <= 4
     return jax.shard_map(
         two_sections(n) if fast else relay_shards,
         mesh=mesh,

time: 47.7 us -> 46.9 us (0.983)
  Pallas kernels: 46.3 us -> 45.5 us
    pallas_call x1, Pallas kernels: 46.3 us -> 45.5 us  [shards(): pl.pallas_call(functools.partial(kernel, n, sizes), out_shape=pltpu.VMEM(...]
where the time goes in v6:
time: 46.9 us; the launch traced here: 46.7 us
  Pallas kernels  45.5 us (97%)
  between operations  0.64 us (1%)
  other arithmetic  0.6 us (1%)
    pallas_call x1, Pallas kernels, shards(): pl.pallas_call(functools.partial(kernel, n, sizes), out_shape=pltpu.VMEM(...  45.5 us

profile of v6, /device:TPU:0, one launch (start us, length us, event | category | flops | bytes accessed | tf_op | source)
XLA Modules:
  0.0 46.7 jit_solution(11228324916668750801)
XLA Ops:
  0.6 45.5 %shard_map.95 = f32[3,2,1,500]{3,2,1,0:T(1,128)S(1)} custom-call(bf16[160,1024]{1,0:T(8,128)(2,1)} %bitcast.16, bf16[64,1536]{1,0:T(8,128)(2,1)} %bitcast.17, bf16[2,64,512]{2,1,0:T(8,128)(2,1)} %bitcast.18, bf16[64,512]{1,0:T(8,128)(2,1)} %bitcast.20, bf16[2,64,512]{2,1,0:T(8,128)(2,1)} %bitcast.19, f32[1,1024]{1,0:T(1,128)} %gain_in.1, ...), custom_call_target="tpu_custom_call" | custom-call | tf_op jit(solution)/shard_map/pallas_call | solution.py:871
  46.1 0.6 %add_bitcast_fusion = (f32[2,1,500]{2,1,0:T(1,128)}, f32[2,1,500]{2,1,0:T(1,128)}) fusion(f32[3,2,1,500]{3,2,1,0:T(1,128)S(1)} %shard_map.95), kind=kLoop, calls=%fused_computation | loop fusion | flops 3000 | bytes 20000 | tf_op jit(solution)/shard_map/add | solution.py:930

commit v7 on v6

--- a/solution.py
+++ b/solution.py
@@ -285,6 +285,38 @@
     scale = 1.0 / joined(streams)
     for s in range(streams):
         att[slot, pl.ds((s * micro + b) * toks, toks), :] = (joined(s) * scale).astype(BF16)
+
+
+def class_attend(sizes, acc):
+    micro, toks, width, hd, tangents = sizes
+    factor = HEAD ** (-0.5)
+    part = 2 * HEAD
+    streams = 1 + tangents
+    images = acc.shape[0] // toks
+    even = lax.broadcasted_iota(jnp.int32, (images, part), 1) < HEAD
+    q = jnp.concatenate([acc[pl.ds(i * toks, 8), pl.ds(0, part)][:1] for i in range(images)], 0)
+    zero = jnp.zeros_like(q)
+    both = jnp.concatenate([jnp.where(even, q, zero), jnp.where(even, zero, q)], 0).astype(BF16)
+    k = acc[:, pl.ds(part, part)].astype(BF16)
+    v = acc[:, pl.ds(2 * part, streams * part)].astype(BF16)
+    scores = dot_t(both, k) * factor
+    image = lax.broadcasted_iota(jnp.int32, scores.shape, 0) % images
+    own = lax.broadcasted_iota(jnp.int32, scores.shape, 1) // toks == image
+    scores = jnp.where(own, scores, -jnp.inf)
+    low = jnp.exp(scores - jnp.max(scores, -1, keepdims=True)).astype(BF16)
+    out = dot(low, jnp.concatenate([v, jnp.ones((acc.shape[0], part), BF16)], 1))
+
+    def joined(s):
+        at = slice(s * part, (s + 1) * part)
+        return jnp.where(even, out[:images, at], out[images:, at])
+
+    scale = 1.0 / joined(streams)
+    parts = [joined(s) * scale for s in range(streams)]
+    blank = jnp.zeros((group_of(sizes) - micro * streams, part), F32)
+    rows = []
+    for p in range(images // micro):
+        rows += [x[p * micro : (p + 1) * micro] for x in parts] + [blank] * (blank.shape[0] > 0)
+    return jnp.concatenate(rows, 0).astype(BF16)
 
 
 def first_out(sizes, tok, place, b_full, att, state):
@@ -767,6 +799,9 @@
         if nz > 2:
             relay(nz - 1)
         project(nz - 1)
+        atc_out[...] = class_attend(sizes, acc)
+        scatter(ATC, lambda p: atc_out, atc_in.at[:, column(place)], other, atc_all)
+
         def give(i):
             target = g.plane[i]
             xfer(ATT, att_out.at[target % 4], att_in.at[:, column(place)], target, other).start()
@@ -777,17 +812,10 @@
             if i == FAR[1]:
                 arrived(LB, b1.at[:, pl.ds(0, 3 * rows), :])
                 far_start(2)
-        firsts = []
-        for p in range(4):
-            for i in range(group):
-                at = pl.ds(i * toks, 16) if i < streams * micro else pl.ds(0, 16)
-                firsts.append(att_out[p, at, :].astype(F32)[:1])
-        atc_out[...] = jnp.concatenate(firsts, 0).astype(BF16)
-        scatter(ATC, lambda p: atc_out, atc_in.at[:, column(place)], other, atc_all)
+        far_pass(0)
         for i in FAR:
             give(i)
         sent.append((ATT, att_out))
-        far_pass(0)
         fresh = []
         blank = jnp.zeros((group - micro, width), F32)
         for p in range(4):

time: 46.9 us -> 46.7 us (level)
  no operation moved by 1% of the time
where the time goes in v7:
time: 46.7 us; the launch traced here: 46.5 us
  Pallas kernels  45.3 us (97%)
  between operations  0.64 us (1%)
  other arithmetic  0.6 us (1%)
    pallas_call x1, Pallas kernels, shards(): pl.pallas_call(functools.partial(kernel, n, sizes), out_shape=pltpu.VMEM(...  45.3 us

profile of v7, /device:TPU:0, one launch (start us, length us, event | category | flops | bytes accessed | tf_op | source)
XLA Modules:
  0.0 46.5 jit_solution(1528883984632772081)
XLA Ops:
  0.6 45.3 %shard_map.95 = f32[3,2,1,500]{3,2,1,0:T(1,128)S(1)} custom-call(bf16[160,1024]{1,0:T(8,128)(2,1)} %bitcast.16, bf16[64,1536]{1,0:T(8,128)(2,1)} %bitcast.17, bf16[2,64,512]{2,1,0:T(8,128)(2,1)} %bitcast.18, bf16[64,512]{1,0:T(8,128)(2,1)} %bitcast.20, bf16[2,64,512]{2,1,0:T(8,128)(2,1)} %bitcast.19, f32[1,1024]{1,0:T(1,128)} %gain_in.1, ...), custom_call_target="tpu_custom_call" | custom-call | tf_op jit(solution)/shard_map/pallas_call | solution.py:899
  45.9 0.6 %add_bitcast_fusion = (f32[2,1,500]{2,1,0:T(1,128)}, f32[2,1,500]{2,1,0:T(1,128)}) fusion(f32[3,2,1,500]{3,2,1,0:T(1,128)S(1)} %shard_map.95), kind=kLoop, calls=%fused_computation | loop fusion | flops 3000 | bytes 20000 | tf_op jit(solution)/shard_map/add | solution.py:958

commit v8 on v7

--- a/solution.py
+++ b/solution.py
@@ -588,7 +588,7 @@
         sent.append((GAIN, gains.at[section]))
         loaded(4, b_full.at[:, own, :])
         gather = Gather(n, g, b_full, b_send, b_recv)
-        lag = 2
+        lag = 1
         gather.along(False)
         for d in range(nz + lag):
             if d < nz:
@@ -809,7 +809,7 @@
         for i in FAR:
             for b in range(micro):
                 first_attend(sizes, acc, att_out, g.plane[i] % 4, b)
-            if i == FAR[1]:
+            if i == FAR[0]:
                 arrived(LB, b1.at[:, pl.ds(0, 3 * rows), :])
                 far_start(2)
         far_pass(0)

time: 46.7 us -> 46.7 us (level)
  no operation moved by 1% of the time
where the time goes in v8:
time: 46.7 us; the launch traced here: 46.5 us
  Pallas kernels  45.3 us (97%)
  between operations  0.64 us (1%)
  other arithmetic  0.6 us (1%)
    pallas_call x1, Pallas kernels, shards(): pl.pallas_call(functools.partial(kernel, n, sizes), out_shape=pltpu.VMEM(...  45.3 us

profile of v8, /device:TPU:0, one launch (start us, length us, event | category | flops | bytes accessed | tf_op | source)
XLA Modules:
  0.0 46.5 jit_solution(18285205711428174178)
XLA Ops:
  0.6 45.3 %shard_map.95 = f32[3,2,1,500]{3,2,1,0:T(1,128)S(1)} custom-call(bf16[160,1024]{1,0:T(8,128)(2,1)} %bitcast.16, bf16[64,1536]{1,0:T(8,128)(2,1)} %bitcast.17, bf16[2,64,512]{2,1,0:T(8,128)(2,1)} %bitcast.18, bf16[64,512]{1,0:T(8,128)(2,1)} %bitcast.20, bf16[2,64,512]{2,1,0:T(8,128)(2,1)} %bitcast.19, f32[1,1024]{1,0:T(1,128)} %gain_in.1, ...), custom_call_target="tpu_custom_call" | custom-call | tf_op jit(solution)/shard_map/pallas_call | solution.py:899
  45.9 0.6 %add_bitcast_fusion = (f32[2,1,500]{2,1,0:T(1,128)}, f32[2,1,500]{2,1,0:T(1,128)}) fusion(f32[3,2,1,500]{3,2,1,0:T(1,128)S(1)} %shard_map.95), kind=kLoop, calls=%fused_computation | loop fusion | flops 3000 | bytes 20000 | tf_op jit(solution)/shard_map/add | solution.py:958
